TPU v7x, 128 devices: a whole 4x4x4 slice. The times are simulated.
128 devices in a mesh: seq: 16 (over y_hi, z, core), tp: 8 (over x, y_lo).
Axes of the slice: x: 4, y: 4 (y_hi: 2, y_lo: 2; y = y_hi * 2 + y_lo), z: 4, core: 2. Of those that a mesh axis runs over, the one named last changes fastest.
Arguments:
- streams: bfloat16 [8192, 4, 4096], P('seq', None, 'tp'), may hold values from -6 to 6
- doc_ids: int32 [8192], P('seq'), may hold values from 0 to 3, never falling along the last dimension, each value on 1 to 4096 neighbouring positions
- mix_weight: float32 [4, 4096, 24], P(None, 'tp'), may hold values from -0.046875 to 0.046875
- mix_bias: float32 [24], replicated, may hold values from -1 to 1
- attn_gain: float32 [4096], replicated, may hold values from 0.1 to 1.9
- w_qkv: bfloat16 [4096, 3, 4096], P(None, None, 'tp'), may hold values from -1 to 1
- w_out: bfloat16 [4096, 4096], P('tp'), may hold values from -0.5 to 0.5
Outputs:
- new_streams: bfloat16 [8192, 4, 4096], P('seq', None, 'tp')
Inputs may be any that keep to these rules, and one draw needn't show every extreme that they name: doc_ids never fall along the sequence; each of the 4 documents has 1 to 4096 positions, and the longest has exactly 4096.
All inputs are finite; a program needn't handle non-finite values.
Results may differ from a plain program's by a relative error of at most 0.014.
The roundings to bfloat16 on the way count: a program that leaves them out, or rounds other values in their place, can miss the bound.
Values may be sent and summed in bfloat16 or wider, within the bound.
A program may use at most 256 MiB of HBM per device.

v0:
```python
import jax
import jax.numpy as jnp
from jax import lax
from jax.experimental import pallas as pl
from jax.experimental.pallas import tpu as pltpu
from jax.sharding import PartitionSpec as P

D = 4096
HD = 128
S = 4
ROUNDS = 20
EPS = 1e-6
T = 512
W = 512
NC = 8
NO = 4
RO = T // NO
HALF = 256
AHEAD = 3
R = T // NC
F32 = jnp.float32
BF = jnp.bfloat16
MESH = pl.DeviceIdType.MESH
NT = (((1,), (1,)), ((), ()))
NEG = -1e30
VMEM = pltpu.VMEM
DMA = pltpu.SemaphoreType.DMA


def where_am_i():
    seq = lax.axis_index("seq")
    tp = lax.axis_index("tp")
    return seq, tp


def remote(src, dst, ssem, rsem, seq, tp):
    return pltpu.make_async_remote_copy(
        src_ref=src, dst_ref=dst, send_sem=ssem, recv_sem=rsem,
        device_id={"seq": seq, "tp": tp}, device_id_type=MESH,
    )


def greet(peers):
    barrier = pltpu.get_barrier_semaphore()
    for seq, tp in peers:
        pl.semaphore_signal(barrier, inc=1, device_id={"seq": seq, "tp": tp}, device_id_type=MESH)
    return lambda: pl.semaphore_wait(barrier, len(peers))


def columns(rows8):
    k = rows8.shape[0]
    if k < 128:
        rows8 = jnp.concatenate([rows8, jnp.zeros((128 - k, rows8.shape[1]), F32)], axis=0)
    return rows8.T


def balanced(e0, e1):
    sub = lax.broadcasted_iota(jnp.int32, e0.shape, 0)
    even, low = sub % 2 == 0, sub % 4 < 2

    def row_total(e):
        u = e + jnp.where(even, pltpu.roll(e, 7, 0), pltpu.roll(e, 1, 0))
        return u + jnp.where(low, pltpu.roll(u, 6, 0), pltpu.roll(u, 2, 0))

    def one_round(_, pair):
        e0, e1 = pair
        e0 = e0 / row_total(e0)
        e1 = e1 / row_total(e1)
        t = e0 + e1
        t = t + pltpu.roll(t, 4, 0)
        return e0 / t, e1 / t

    return lax.fori_loop(0, ROUNDS, one_round, (e0, e1))


def first_kernel(
    x_hbm, docs_hbm, wmix_hbm, bias_hbm, gain_hbm, w_hbm,
    att, mix_cols, counts,
    xraw, xs, docs, wmix, bias, gain,
    wbuf, g, sb, gained, unow, urecv, nall, nrecv, csend, crecv, pre_cols,
    x_sem, i_sem, w_sem, u_ss, u_rs, n_ss, n_rs, c_ss, c_rs, g_ss, g_rs, a_ss, a_rs, o_sem,
    sib_ss, sib_rs, x_ss, x_rs, sib2_ss, sib2_rs,
):
    seq, tp = where_am_i()
    yhi, z, core = seq // 8, (seq // 2) % 4, seq % 2
    x, y = tp // 2, tp % 2
    sibling, mirror = seq + 1 - 2 * core, (seq + 8) % 16
    tp_peers = [(seq, (tp + r) % 8) for r in range(1, 8)]
    z_peers = [yhi * 8 + ((z + d) % 4) * 2 + core for d in range(1, 4)]
    entered = greet(tp_peers + [(p, tp) for p in z_peers] + [(sibling, tp), (mirror, tp)])

    small = [
        pltpu.make_async_copy(a, b, i_sem.at[i])
        for i, (a, b) in enumerate(
            ((wmix_hbm, wmix), (docs_hbm, docs), (bias_hbm, bias), (gain_hbm, gain))
        )
    ]
    parts_of_x = [
        pltpu.make_async_copy(x_hbm.at[pl.ds(q * 128, 128)], xraw.at[pl.ds(q * 128, 128)], x_sem.at[q])
        for q in range(4)
    ]
    small[0].start()
    for q in range(4):
        parts_of_x[q].start()
    for k in range(1, 4):
        small[k].start()

    def wcopy(i):
        return pltpu.make_async_copy(w_hbm.at[i], wbuf.at[i], w_sem.at[i])

    small[0].wait()
    parts = []
    for s in range(S):
        w = jnp.concatenate([wmix[s], jnp.zeros((8, W), F32)], axis=0)
        hi = w.astype(BF).astype(F32)
        mid = (w - hi).astype(BF).astype(F32)
        low = (w - hi) - mid
        parts.append(jnp.concatenate([hi, mid, low], axis=0).astype(BF))
    sub = lax.broadcasted_iota(jnp.int32, (8, 128), 0)
    for q in range(4):
        rows = slice(q * 128, (q + 1) * 128)
        parts_of_x[q].wait()
        if q == 3:
            for i in range(3):
                wcopy(i).start()
        xs[:, rows, :] = jnp.swapaxes(xraw[rows], 0, 1)
        acc = jnp.zeros((128, 128), F32)
        logits = jnp.zeros((32, 128), F32)
        for s in range(S):
            xv = xs[s, rows, :]
            got = lax.dot_general(parts[s], xv, NT, preferred_element_type=F32)
            logits = logits + (got[0:32] + (got[32:64] + got[64:96]))
            x32 = xv.astype(F32)
            sq = x32 * x32
            acc = acc + ((sq[:, 0:128] + sq[:, 128:256]) + (sq[:, 256:384] + sq[:, 384:512]))
        squares = jnp.sum(acc.T, axis=0, keepdims=True)
        unow[:, rows] = jnp.where(
            sub < 4, logits[0:8], jnp.where(sub == 4, jnp.broadcast_to(squares, (8, 128)), 0.0)
        )
        nall[:, rows] = logits[0:24]

    entered()
    for r, (sq_, tp_) in enumerate(tp_peers):
        remote(unow, urecv.at[r], u_ss.at[r], u_rs.at[r], sq_, tp_).start()

    for k in range(1, 4):
        small[k].wait()
    dv = docs[...]
    cv = jnp.zeros((8, 128), jnp.int32)
    for k in range(1, 4):
        n = jnp.sum(jnp.where(dv < k, 1, 0), axis=1, keepdims=True)
        n = jnp.sum(n, axis=0, keepdims=True)
        cv = jnp.where(sub == k, jnp.broadcast_to(n, (8, 128)), cv)
    csend[0] = cv
    diag = lax.broadcasted_iota(jnp.int32, (24, 24), 0) == lax.broadcasted_iota(jnp.int32, (24, 24), 1)
    bias_col = jnp.sum(jnp.where(diag, jnp.broadcast_to(bias[...], (24, 24)), 0.0), axis=1, keepdims=True)

    def count_to(level, k, to):
        return remote(csend.at[level], crecv.at[k], c_ss.at[k], c_rs.at[k], to, tp)

    total = unow[...]
    for r, (sq_, tp_) in enumerate(tp_peers):
        remote(unow, urecv.at[r], u_ss.at[r], u_rs.at[r], sq_, tp_).wait_recv()
        total = total + urecv[r]
    inv_rms = lax.rsqrt(total[4:5] / (S * D) + EPS)
    pre = 1.0 / (1.0 + jnp.exp(-(total * inv_rms + bias_col[0:8])))
    pre_cols[...] = columns(pre)

    right = ((x + 1) % 4) * 2 + y
    left = ((x + 3) % 4) * 2 + y
    other_y = x * 2 + 1 - y
    b_p = other_y
    b_l0, b_l1 = left, ((x + 3) % 4) * 2 + 1 - y
    b_r0, b_r1 = right, ((x + 1) % 4) * 2 + 1 - y
    b_f0, b_f1 = ((x + 2) % 4) * 2 + y, ((x + 2) % 4) * 2 + 1 - y

    def move(c, k, blk, role, to):
        return remote(g.at[c, blk], g.at[c, blk], g_ss.at[c, k], g_rs.at[c, role], seq, to)

    def arrived(c, role, blk):
        move(c, 0, blk, role, right).wait_recv()

    def make_chunk(c):
        rows = slice(c * R, (c + 1) * R)
        v = pre_cols[rows, 0:1] * xs[0, rows, :].astype(F32)
        for s in range(1, S):
            v = v + pre_cols[rows, s : s + 1] * xs[s, rows, :].astype(F32)
        g[c, tp] = v.astype(BF)

    def send_chunk(c):
        move(c, 2, tp, 0, other_y).start()
        move(c, 0, tp, 1, right).start()
        move(c, 1, tp, 3, left).start()

    make_chunk(0)
    for c in range(NC):
        if c + 1 < NC:
            make_chunk(c + 1)
        if c < AHEAD:
            send_chunk(c)
    for d in range(3):
        count_to(0, d, z_peers[d]).start()
    for i in range(3):
        wcopy(i).wait()

    def block_of(half, d):
        return half * 8 + ((z + 4 - d) % 4) * 2 + core

    def spread(c, d):
        return remote(
            sb.at[(z + d) % 4, c], att.at[seq, c], a_ss.at[c, d - 1], a_rs.at[c, d - 1], z_peers[d - 1], tp,
        )

    def spread_in(c, d):
        remote(
            sb.at[z, c], att.at[block_of(yhi, d), c], a_ss.at[c, d - 1], a_rs.at[c, d - 1], z_peers[d - 1], tp
        ).wait_recv()

    def kept(c):
        return pltpu.make_async_copy(sb.at[z, c], att.at[seq, c], o_sem.at[c])

    def kv(c, d):
        return sb.at[z, c, pl.ds(0, 2)] if d == 0 else att.at[block_of(yhi, d), c, pl.ds(0, 2)]

    def twin(c, d):
        dst = att.at[block_of(yhi, d), c, pl.ds(0, 2)]
        return remote(kv(c, d), dst, sib_ss.at[c, d], sib_rs.at[c, d], sibling, tp)

    def twin_in(c, d):
        dst = att.at[yhi * 8 + ((z + 4 - d) % 4) * 2 + 1 - core, c, pl.ds(0, 2)]
        return remote(kv(c, d), dst, sib_ss.at[c, d], sib_rs.at[c, d], sibling, tp)

    def cross(c, d):
        dst = att.at[block_of(0, d), c, pl.ds(0, 2)]
        return remote(kv(c, d), dst, x_ss.at[c, d], x_rs.at[c, d], mirror, tp)

    def twin2(c, d):
        ref = att.at[block_of(0, d), c, pl.ds(0, 2)]
        return remote(ref, ref, sib2_ss.at[c, d], sib2_rs.at[c, d], sibling, tp)

    def twin2_in(c, d):
        dst = att.at[((z + 4 - d) % 4) * 2 + 1 - core, c, pl.ds(0, 2)]
        return remote(dst, dst, sib2_ss.at[c, d], sib2_rs.at[c, d], sibling, tp)

    def hand_on(i):
        arrived(i, 0, b_p)
        move(i, 3, b_p, 2, right).start()
        move(i, 4, b_p, 4, left).start()

    hand_on(0)

    def step(i, carry):
        @pl.when(i + AHEAD < NC)
        def _():
            send_chunk(i + AHEAD)

        @pl.when(i + 1 < NC)
        def _():
            hand_on(i + 1)

        @pl.when(i < NC)
        def _():
            arrived(i, 1, b_l0)
            move(i, 5, b_l0, 5, right).start()
            arrived(i, 4, b_r1)
            move(i, 6, b_r1, 6, left).start()

        @pl.when((i >= 3) & (i <= NC + 2))
        def _():
            c = i - 3
            for d in range(4):
                if d:
                    spread_in(c, d)

                @pl.when(yhi == 0)
                def _():
                    cross(c, d).start()

                twin(c, d).start()

        @pl.when((i >= 5) & (yhi == 1))
        def _():
            for d in range(4):
                cross(i - 5, d).wait_recv()
                twin2(i - 5, d).start()

        @pl.when((i >= 1) & (i <= NC))
        def _():
            c = i - 1
            arrived(c, 2, b_l1)
            arrived(c, 3, b_r0)
            arrived(c, 5, b_f0)
            arrived(c, 6, b_f1)
            ss = jnp.zeros((R, 128), F32)
            for b in range(8):
                g32 = g[c, b].astype(F32)
                q = g32 * g32
                ss = ss + ((q[:, 0:128] + q[:, 128:256]) + (q[:, 256:384] + q[:, 384:512]))
                gained[:, b * W : (b + 1) * W] = (g32 * gain[:, b * W : (b + 1) * W]).astype(BF)
            norm = lax.rsqrt(jnp.sum(ss, axis=1, keepdims=True) / D + EPS)
            lhs = gained[...]
            for slot, third in ((0, 1), (1, 2), (2, 0)):
                acc = jnp.dot(lhs, wbuf[third], preferred_element_type=F32)
                out = (acc * norm).astype(BF)
                for h in range(4):
                    sb[h, c, slot] = out[:, h * HD : (h + 1) * HD]
            for d in (2, 1, 3):
                spread(c, d).start()
            kept(c).start()

        @pl.when(i == NC)
        def _():
            for r, (sq_, tp_) in enumerate(tp_peers):
                remote(nall, nrecv.at[r], n_ss.at[r], n_rs.at[r], sq_, tp_).start()

        @pl.when(i == 3)
        def _():
            v = csend[0]
            for d in range(3):
                count_to(0, d, z_peers[d]).wait_recv()
                v = v + crecv[d]
            csend[1] = v

        @pl.when(i == 4)
        def _():
            count_to(1, 3, sibling).start()

        @pl.when(i == 5)
        def _():
            count_to(1, 3, sibling).wait_recv()
            csend[2] = csend[1] + crecv[3]

        @pl.when(i == 6)
        def _():
            count_to(2, 4, mirror).start()

        return carry

    lax.fori_loop(0, NC + 3, step, 0)

    count_to(2, 4, mirror).wait_recv()
    counts[...] = csend[2] + crecv[4]
    ztot = nall[...]
    for r, (sq_, tp_) in enumerate(tp_peers):
        remote(nall, nrecv.at[r], n_ss.at[r], n_rs.at[r], sq_, tp_).wait_recv()
        ztot = ztot + nrecv[r]
    ztot = ztot * inv_rms + bias_col
    post = 2.0 / (1.0 + jnp.exp(-ztot[0:8]))
    e0, e1 = balanced(jnp.exp(ztot[8:16]), jnp.exp(ztot[16:24]))
    mix_cols[...] = columns(jnp.concatenate([post, e0, e1], axis=0))

    @pl.when(yhi == 1)
    def _():
        def tail(c, carry):
            for d in range(4):
                cross(c, d).wait_recv()
                twin2(c, d).start()
            return carry

        lax.fori_loop(NC - 2, NC, tail, 0)

    for r, (sq_, tp_) in enumerate(tp_peers):
        remote(unow, urecv.at[r], u_ss.at[r], u_rs.at[r], sq_, tp_).wait_send()
        remote(nall, nrecv.at[r], n_ss.at[r], n_rs.at[r], sq_, tp_).wait_send()
    for d in range(3):
        count_to(0, d, z_peers[d]).wait_send()
    count_to(1, 3, sibling).wait_send()
    count_to(2, 4, mirror).wait_send()

    def drain(c, carry):
        for k in range(7):
            move(c, k, tp, 0, right).wait_send()
        kept(c).wait()
        for d in range(1, 4):
            spread(c, d).wait_send()
        for d in range(4):
            twin(c, d).wait_send()
            twin_in(c, d).wait_recv()

        @pl.when(yhi == 0)
        def _():
            for d in range(4):
                cross(c, d).wait_send()

        @pl.when(yhi == 1)
        def _():
            for d in range(4):
                twin2(c, d).wait_send()
                twin2_in(c, d).wait_recv()

        return carry

    lax.fori_loop(0, NC, drain, 0)


def attention_kernel(att_hbm, cnt_hbm, ctx, att, cnt, vx, m_ref, acc_ref, c_sem, k_sem, v_sem, q_sem):
    seq = lax.axis_index("seq")
    yhi, core = seq // 8, seq % 2
    counts_in = pltpu.make_async_copy(cnt_hbm, cnt, c_sem)
    counts_in.start()

    def q_in(qi):
        qb = yhi * 8 + qi * 2 + core
        return pltpu.make_async_copy(att_hbm.at[qb, :, 2], att.at[qb, :, 2], q_sem.at[qi])

    def k_in(kb):
        return pltpu.make_async_copy(att_hbm.at[kb, :, 0], att.at[kb, :, 0], k_sem.at[kb])

    def v_in(kb):
        return pltpu.make_async_copy(att_hbm.at[kb, :, 1], vx.at[kb, :, :, pl.ds(0, HD)], v_sem.at[kb])

    q_in(0).start()
    counts_in.wait()
    starts = [cnt[k, 0] for k in range(1, 4)]
    scale = HD ** (-0.5) * 1.4426950408889634

    def start_of(p):
        v = p * 0
        for c in starts:
            v = jnp.where(c <= p, jnp.maximum(v, c), v)
        return v

    first_needed = start_of((yhi * 8 + core) * T) // T

    def fetch(kb, c):
        k_in(kb).start()
        v_in(kb).start()
        return c

    def land(kb, c):
        k_in(kb).wait()
        v_in(kb).wait()
        return c

    lax.fori_loop(first_needed, yhi * 8 + core + 1, fetch, 0)
    for qi in range(1, 4):
        q_in(qi).start()
    lax.fori_loop(yhi * 8 + core + 1, yhi * 8 + core + 7, fetch, 0)

    def ones(kb, c):
        vx[kb, :, :, HD:] = jnp.ones((NC, R, HD), BF)
        return c

    lax.fori_loop(first_needed, yhi * 8 + core + 7, ones, 0)

    def one_query_block(qi, carry):
        qb = yhi * 8 + qi * 2 + core
        lax.fori_loop(jnp.where(qi == 0, first_needed, qb - 1), qb + 1, land, 0)
        q_in(qi).wait()
        q = att[qb, :, 2].reshape(T, HD)
        first = start_of(qb * T)
        last = start_of(qb * T + T - 1)
        lo = first // T
        mid = jnp.minimum((last + T - 1) // T, qb)
        qpos = qb * T + lax.broadcasted_iota(jnp.int32, (T, 1), 0)
        qstart = start_of(qpos)
        def block(kb, mode, n=1):
            k = att[pl.ds(kb, n), :, 0].reshape(n * T, HD)
            v = vx[pl.ds(kb, n)].reshape(n * T, 2 * HD)

            def scores(t):
                rows = slice(t * HALF, (t + 1) * HALF)
                s = lax.dot_general(q[rows], k, NT, preferred_element_type=F32)
                if mode != "all":
                    kpos = kb * T + lax.broadcasted_iota(jnp.int32, (1, T), 1)
                    ok = kpos >= qstart[rows]
                    if mode == "diagonal":
                        ok = ok & (kpos <= qpos[rows])
                    s = jnp.where(ok, s, NEG)
                return s

            later = scores(0)
            for t in range(T // HALF):
                rows = slice(t * HALF, (t + 1) * HALF)
                s = later
                if (t + 1) * HALF < T:
                    later = scores(t + 1)
                top = s[:, 0:128]
                for e in range(1, n * 4):
                    top = jnp.maximum(top, s[:, e * 128 : (e + 1) * 128])
                m_new = jnp.max(top, axis=1, keepdims=True)
                if mode != "diagonal":
                    m_old = m_ref[rows, 0:1]
                    m_new = jnp.maximum(m_old, m_new)
                    alpha = jnp.exp2((m_old - m_new) * scale)
                p = jnp.exp2((s - m_new) * scale).astype(BF)
                more = jnp.dot(p, v, preferred_element_type=F32)
                acc_ref[rows] = more if mode == "diagonal" else acc_ref[rows] * alpha + more
                m_ref[rows] = jnp.broadcast_to(m_new, (HALF, 128))

        def some(kb, c):
            block(kb, "start")
            return c

        def two(k, c):
            block(mid + 2 * k, "all", 2)
            return c

        def one(kb, c):
            block(kb, "all")
            return c

        block(qb, "diagonal")
        lax.fori_loop(lo, mid, some, 0)
        pairs = (qb - mid) // 2
        lax.fori_loop(0, pairs, two, 0)
        lax.fori_loop(mid + 2 * pairs, qb, one, 0)
        out = acc_ref[:, 0:HD] / acc_ref[:, HD : HD + 1]
        ctx[qi] = out.astype(BF).reshape(NO, RO, HD)
        return carry

    lax.fori_loop(0, 4, one_query_block, 0)


def last_kernel(
    ctx_hbm, w_hbm,
    branch,
    ctx, wbuf, cbuf, snd, snh, own, rcv, rch,
    c_sem, w_sem, z_ss, z_rs, s_ss, s_rs, h_ss, h_rs,
):
    seq, tp = where_am_i()
    yhi, z, core = seq // 8, (seq // 2) % 4, seq % 2
    x, y = tp // 2, tp % 2
    right = ((x + 1) % 4) * 2 + y
    left = ((x + 3) % 4) * 2 + y
    other_y = x * 2 + 1 - y
    z_peers = [yhi * 8 + ((z + d) % 4) * 2 + core for d in range(1, 4)]
    entered = greet([(p, tp) for p in z_peers] + [(seq, right), (seq, left), (seq, other_y)])
    ccopy = pltpu.make_async_copy(ctx_hbm, ctx, c_sem)
    ccopy.start()
    wcopy = pltpu.make_async_copy(w_hbm, wbuf, w_sem)
    wcopy.start()
    ccopy.wait()
    entered()

    def back(c, d):
        return remote(
            ctx.at[(z + d) % 4, c], cbuf.at[z, c], z_ss.at[c, d - 1], z_rs.at[c, d - 1], z_peers[d - 1], tp
        )

    def back_in(c, d):
        remote(
            ctx.at[z, c], cbuf.at[(z + 4 - d) % 4, c], z_ss.at[c, d - 1], z_rs.at[c, d - 1], z_peers[d - 1], tp
        ).wait_recv()

    for c in range(NO):
        for d in (2, 1, 3):
            back(c, d).start()
    cbuf[z] = ctx[z]
    wcopy.wait()

    def pass_on(c, k, to):
        return remote(snd.at[c, k], rcv.at[c, k], s_ss.at[c, k], s_rs.at[c, k], seq, to)

    def half(c, k, to):
        return remote(snh.at[c, k], rch.at[c, k], h_ss.at[c, k], h_rs.at[c, k], seq, to)

    to_right, to_left, far = ((x + 1) % 4) * 2, ((x + 3) % 4) * 2, ((x + 2) % 4) * 2

    def project(c, carry):
        for d in range(1, 4):
            back_in(c, d)
        lhs = jnp.concatenate([cbuf[h, c] for h in range(4)], axis=1)

        def term(b):
            cols = pl.ds(pl.multiple_of(b * W, W), W)
            return jnp.dot(lhs, wbuf[:, cols], preferred_element_type=F32)

        snd[c, 0] = term(far + 1 - y).astype(BF)
        snd[c, 1] = term(to_right + 1 - y).astype(BF)
        pass_on(c, 0, other_y).start()
        snd[c, 2] = term(to_left + 1 - y).astype(BF)
        pass_on(c, 1, right).start()
        own[c, 0] = term(far + y)
        pass_on(c, 2, left).start()
        own[c, 1] = term(to_right + y)
        own[c, 2] = term(to_left + y)
        own[c, 3] = term(other_y)
        own[c, 4] = term(tp)
        return carry

    lax.fori_loop(0, NO, project, 0)

    def second(c, carry):
        pass_on(c, 0, other_y).wait_recv()
        far_sum = (own[c, 0] + rcv[c, 0].astype(F32)).astype(BF)
        snh[c, 0] = far_sum[0 : RO // 2]
        snh[c, 1] = far_sum[RO // 2 :]
        half(c, 0, right).start()
        half(c, 1, left).start()
        return carry

    lax.fori_loop(0, NO, second, 0)

    def third(c, carry):
        pass_on(c, 1, right).wait_recv()
        pass_on(c, 2, left).wait_recv()
        snd[c, 5] = (own[c, 3] + (rcv[c, 1].astype(F32) + rcv[c, 2].astype(F32))).astype(BF)
        pass_on(c, 5, other_y).start()
        half(c, 0, right).wait_recv()
        snd[c, 3, 0 : RO // 2] = (own[c, 1, 0 : RO // 2] + rch[c, 0].astype(F32)).astype(BF)
        snd[c, 3, RO // 2 :] = own[c, 1, RO // 2 :].astype(BF)
        pass_on(c, 3, right).start()
        half(c, 1, left).wait_recv()
        snd[c, 4, 0 : RO // 2] = own[c, 2, 0 : RO // 2].astype(BF)
        snd[c, 4, RO // 2 :] = (own[c, 2, RO // 2 :] + rch[c, 1].astype(F32)).astype(BF)
        pass_on(c, 4, left).start()
        return carry

    lax.fori_loop(0, NO, third, 0)

    def fourth(c, carry):
        pass_on(c, 5, other_y).wait_recv()
        pass_on(c, 3, right).wait_recv()
        pass_on(c, 4, left).wait_recv()
        rows = pl.ds(pl.multiple_of(c * RO, RO), RO)
        branch[rows, :] = (own[c, 4] + rcv[c, 5].astype(F32)) + (
            rcv[c, 3].astype(F32) + rcv[c, 4].astype(F32)
        )
        return carry

    lax.fori_loop(0, NO, fourth, 0)

    def drain(c, carry):
        for d in range(1, 4):
            back(c, d).wait_send()
        for k in range(6):
            pass_on(c, k, right).wait_send()
        half(c, 0, right).wait_send()
        half(c, 1, left).wait_send()
        return carry

    lax.fori_loop(0, NO, drain, 0)


def combine_kernel(xraw, cols, branch, out):
    xv = jnp.swapaxes(xraw[...], 0, 1)
    wide = [xv[j].astype(F32) for j in range(S)]
    b = branch[...]
    new = []
    for i in range(S):
        v = cols[:, 4 + i : 5 + i] * b
        for j in range(S):
            k = 8 + 4 * i + j
            v = v + cols[:, k : k + 1] * wide[j]
        new.append(v.astype(BF))
    out[...] = jnp.swapaxes(jnp.stack(new, axis=0), 0, 1)


def local(streams, doc_ids, mix_weight, mix_bias, attn_gain, w_qkv, w_out):
    wmix = jnp.transpose(mix_weight, (0, 2, 1))
    wq = jnp.transpose(w_qkv, (1, 0, 2))
    vm = pl.BlockSpec(memory_space=VMEM)
    hbm = pl.BlockSpec(memory_space=pl.ANY)
    sds = jax.ShapeDtypeStruct
    att, mix_cols, counts = pl.pallas_call(
        first_kernel,
        name="gather_project",
        out_shape=(
            sds((16, NC, 3, R, HD), BF),
            sds((T, 128), F32),
            sds((8, 128), jnp.int32),
        ),
        in_specs=[hbm] * 6,
        out_specs=(hbm, vm, vm),
        scratch_shapes=[
            VMEM((T, S, W), BF),
            VMEM((S, T, W), BF),
            VMEM((4, 128), jnp.int32),
            VMEM((S, 24, W), F32),
            VMEM((1, 24), F32),
            VMEM((1, D), F32),
            VMEM((3, D, W), BF),
            VMEM((NC, 8, R, W), BF),
            VMEM((4, NC, 3, R, HD), BF),
            VMEM((R, D), BF),
            VMEM((8, T), F32),
            VMEM((7, 8, T), F32),
            VMEM((24, T), F32),
            VMEM((7, 24, T), F32),
            VMEM((3, 8, 128), jnp.int32),
            VMEM((5, 8, 128), jnp.int32),
            VMEM((T, 128), F32),
            DMA((4,)),
            DMA((4,)),
            DMA((3,)),
            DMA((7,)), DMA((7,)),
            DMA((7,)), DMA((7,)),
            DMA((5,)), DMA((5,)),
            DMA((NC, 7)), DMA((NC, 7)),
            DMA((NC, 3)), DMA((NC, 3)),
            DMA((NC,)),
            DMA((NC, 4)), DMA((NC, 4)),
            DMA((NC, 4)), DMA((NC, 4)),
            DMA((NC, 4)), DMA((NC, 4)),
        ],
        compiler_params=pltpu.CompilerParams(
            collective_id=0, has_side_effects=True, vmem_limit_bytes=60 * 1024 * 1024
        ),
    )(
        streams, doc_ids.reshape(4, 128), wmix, mix_bias.reshape(1, 24), attn_gain.reshape(1, D), wq,
    )
    ctx = pl.pallas_call(
        attention_kernel,
        name="attention",
        out_shape=sds((4, NO, RO, HD), BF),
        in_specs=[hbm, hbm],
        out_specs=vm,
        scratch_shapes=[
            VMEM((16, NC, 3, R, HD), BF),
            pltpu.SMEM((8, 128), jnp.int32),
            VMEM((16, NC, R, 2 * HD), BF),
            VMEM((T, 128), F32), VMEM((T, 2 * HD), F32),
            DMA(()), DMA((16,)), DMA((16,)), DMA((4,)),
        ],
        compiler_params=pltpu.CompilerParams(vmem_limit_bytes=60 * 1024 * 1024),
    )(att, counts)
    branch = pl.pallas_call(
        last_kernel,
        name="project_out",
        out_shape=sds((T, W), F32),
        in_specs=[hbm, hbm],
        out_specs=vm,
        scratch_shapes=[
            VMEM((4, NO, RO, HD), BF),
            VMEM((W, D), BF),
            VMEM((4, NO, RO, HD), BF),
            VMEM((NO, 6, RO, W), BF),
            VMEM((NO, 2, RO // 2, W), BF),
            VMEM((NO, 5, RO, W), F32),
            VMEM((NO, 6, RO, W), BF),
            VMEM((NO, 2, RO // 2, W), BF),
            DMA(()),
            DMA(()),
            DMA((NO, 3)), DMA((NO, 3)),
            DMA((NO, 6)), DMA((NO, 6)),
            DMA((NO, 2)), DMA((NO, 2)),
        ],
        compiler_params=pltpu.CompilerParams(
            collective_id=1, has_side_effects=True, vmem_limit_bytes=60 * 1024 * 1024
        ),
    )(ctx, w_out)
    return pl.pallas_call(
        combine_kernel,
        name="combine",
        grid=(4,),
        out_shape=sds((T, S, W), BF),
        in_specs=[
            pl.BlockSpec((T // 4, S, W), lambda i: (i, 0, 0)),
            pl.BlockSpec((T // 4, 128), lambda i: (i, 0)),
            pl.BlockSpec((T // 4, W), lambda i: (i, 0)),
        ],
        out_specs=pl.BlockSpec((T // 4, S, W), lambda i: (i, 0, 0)),
        compiler_params=pltpu.CompilerParams(vmem_limit_bytes=60 * 1024 * 1024),
    )(streams, mix_cols, branch)


def solution(mesh):
    in_specs = (
        P("seq", None, "tp"),
        P("seq"),
        P(None, "tp", None),
        P(),
        P(),
        P(None, None, "tp"),
        P("tp", None),
    )
    return jax.shard_map(
        local, mesh=mesh, in_specs=in_specs, out_specs=P("seq", None, "tp"), check_vma=False
    )
```

profile of v0, /device:TPU:16, one launch (start us, length us, event | category | flops | bytes accessed | tf_op | source)
XLA Modules:
  0.0 129.7 jit_solution(7842688155759138448)
XLA Ops:
  0.0 69.4 %gather_project.1 = (bf16[16,8,3,64,128]{4,3,2,1,0:T(8,128)(2,1)}, f32[512,128]{1,0:T(8,128)}, s32[8,128]{1,0:T(8,128)}) custom-call(bf16[512,4,512]{2,1,0:T(4,128)(2,1)} %xraw.1, s32[4,128]{1,0:T(4,128)} %bitcast.8, f32[4,24,512]{2,1,0:T(8,128)} %bitcast.6, f32[1,24]{1,0:T(1,128)} %bitcast.9, f32[1,4096]{1,0:T(1,128)} %bitcast.7, bf16[3,4096,512]{2,1,0:T(8,128)(2,1)} %bitcast.5), custom_call_target="tpu_custom_call" | custom-call | tf_op jit(solution)/shard_map/gather_project/pallas_call | solution.py:656
  69.4 19.9 %attention.1.ctx_hbm = bf16[4,4,128,128]{3,2,1,0:T(8,128)(2,1)} custom-call(bf16[16,8,3,64,128]{4,3,2,1,0:T(8,128)(2,1)} %get-tuple-element.9.att_hbm, s32[8,128]{1,0:T(8,128)} %get-tuple-element.10.cnt_hbm), custom_call_target="tpu_custom_call" | custom-call | tf_op jit(solution)/shard_map/attention/pallas_call | solution.py:703
  89.3 35.1 %project_out.1.branch = f32[512,512]{1,0:T(8,128)} custom-call(bf16[4,4,128,128]{3,2,1,0:T(8,128)(2,1)} %attention.1.ctx_hbm, bf16[512,4096]{1,0:T(8,128)(2,1)} %w_hbm.1), custom_call_target="tpu_custom_call" | custom-call | tf_op jit(solution)/shard_map/project_out/pallas_call | solution.py:718
  124.4 5.3 %combine.1 = bf16[512,4,512]{2,1,0:T(4,128)(2,1)} custom-call(bf16[512,4,512]{2,1,0:T(4,128)(2,1)} %xraw.1, f32[512,128]{1,0:T(8,128)} %get-tuple-element.8.cols, f32[512,512]{1,0:T(8,128)} %project_out.1.branch), custom_call_target="tpu_custom_call" | custom-call | tf_op jit(solution)/shard_map/combine/pallas_call | solution.py:743
where the time goes:
time: 131 us; the launch traced here: 130 us
  Pallas kernels  130 us (99%)
    pallas_call x1, Pallas kernels, local(): pl.pallas_call(first_kernel, name='gather_project', out_shape=(sds((16, N...  69.4 us
    pallas_call x1, Pallas kernels, local(): pl.pallas_call(last_kernel, name='project_out', out_shape=sds((T, W), F32...  35.1 us
    pallas_call x1, Pallas kernels, local(): pl.pallas_call(attention_kernel, name='attention', out_shape=sds((4, NO,...  19.9 us
    pallas_call x1, Pallas kernels, local(): pl.pallas_call(combine_kernel, name='combine', grid=(4,), out_shape=sds((...  5.32 us

commit v1 on v0

--- a/solution.py
+++ b/solution.py
@@ -15,6 +15,8 @@
 NC = 8
 NO = 4
 RO = T // NO
+BLOCKS = 160
+TILES = 9216
 HALF = 256
 AHEAD = 3
 R = T // NC
@@ -77,8 +79,8 @@
     x_hbm, docs_hbm, wmix_hbm, bias_hbm, gain_hbm, w_hbm,
     att, mix_cols, counts,
     xraw, xs, docs, wmix, bias, gain,
-    wbuf, g, sb, gained, unow, urecv, nall, nrecv, csend, crecv, pre_cols,
-    x_sem, i_sem, w_sem, u_ss, u_rs, n_ss, n_rs, c_ss, c_rs, g_ss, g_rs, a_ss, a_rs, o_sem,
+    wbuf, g, sb, gained, norms, unow, urecv, nall, nrecv, csend, crecv, pre_cols,
+    x_sem, i_sem, w_sem, u_ss, u_rs, n_ss, n_rs, c_ss, c_rs, g_ss, g_rs, a_ss, a_rs, q_ss, q_rs, o_sem, t_sem,
     sib_ss, sib_rs, x_ss, x_rs, sib2_ss, sib2_rs,
 ):
     seq, tp = where_am_i()
@@ -206,14 +208,30 @@
     def block_of(half, d):
         return half * 8 + ((z + 4 - d) % 4) * 2 + core
 
+    two = pl.ds(0, 2)
+
     def spread(c, d):
         return remote(
-            sb.at[(z + d) % 4, c], att.at[seq, c], a_ss.at[c, d - 1], a_rs.at[c, d - 1], z_peers[d - 1], tp,
+            sb.at[(z + d) % 4, c, two], att.at[seq, c, two],
+            a_ss.at[c, d - 1], a_rs.at[c, d - 1], z_peers[d - 1], tp,
         )
 
     def spread_in(c, d):
         remote(
-            sb.at[z, c], att.at[block_of(yhi, d), c], a_ss.at[c, d - 1], a_rs.at[c, d - 1], z_peers[d - 1], tp
+            sb.at[z, c, two], att.at[block_of(yhi, d), c, two],
+            a_ss.at[c, d - 1], a_rs.at[c, d - 1], z_peers[d - 1], tp,
+        ).wait_recv()
+
+    def spread_q(c, d):
+        return remote(
+            sb.at[(z + d) % 4, c, 2], att.at[seq, c, 2],
+            q_ss.at[c, d - 1], q_rs.at[c, d - 1], z_peers[d - 1], tp,
+        )
+
+    def spread_q_in(c, d):
+        remote(
+            sb.at[z, c, 2], att.at[block_of(yhi, d), c, 2],
+            q_ss.at[c, d - 1], q_rs.at[c, d - 1], z_peers[d - 1], tp,
         ).wait_recv()
 
     def kept(c):
@@ -249,7 +267,7 @@
 
     hand_on(0)
 
-    def step(i, carry):
+    def feed(i):
         @pl.when(i + AHEAD < NC)
         def _():
             send_chunk(i + AHEAD)
@@ -265,28 +283,10 @@
             arrived(i, 4, b_r1)
             move(i, 6, b_r1, 6, left).start()
 
-        @pl.when((i >= 3) & (i <= NC + 2))
-        def _():
-            c = i - 3
-            for d in range(4):
-                if d:
-                    spread_in(c, d)
-
-                @pl.when(yhi == 0)
-                def _():
-                    cross(c, d).start()
-
-                twin(c, d).start()
-
-        @pl.when((i >= 5) & (yhi == 1))
-        def _():
-            for d in range(4):
-                cross(i - 5, d).wait_recv()
-                twin2(i - 5, d).start()
-
-        @pl.when((i >= 1) & (i <= NC))
-        def _():
-            c = i - 1
+    def projected(c0):
+        for e in range(2):
+            c = c0 + e
+            rows = slice(e * R, (e + 1) * R)
             arrived(c, 2, b_l1)
             arrived(c, 3, b_r0)
             arrived(c, 5, b_f0)
@@ -296,24 +296,71 @@
                 g32 = g[c, b].astype(F32)
                 q = g32 * g32
                 ss = ss + ((q[:, 0:128] + q[:, 128:256]) + (q[:, 256:384] + q[:, 384:512]))
-                gained[:, b * W : (b + 1) * W] = (g32 * gain[:, b * W : (b + 1) * W]).astype(BF)
-            norm = lax.rsqrt(jnp.sum(ss, axis=1, keepdims=True) / D + EPS)
-            lhs = gained[...]
-            for slot, third in ((0, 1), (1, 2), (2, 0)):
-                acc = jnp.dot(lhs, wbuf[third], preferred_element_type=F32)
-                out = (acc * norm).astype(BF)
-                for h in range(4):
-                    sb[h, c, slot] = out[:, h * HD : (h + 1) * HD]
+                gained[rows, b * W : (b + 1) * W] = (g32 * gain[:, b * W : (b + 1) * W]).astype(BF)
+            norms[rows, :] = jnp.broadcast_to(
+                lax.rsqrt(jnp.sum(ss, axis=1, keepdims=True) / D + EPS), (R, 128)
+            )
+        norm = norms[:, 0:1]
+        lhs = gained[...]
+
+        def project(slot, third):
+            out = (jnp.dot(lhs, wbuf[third], preferred_element_type=F32) * norm).astype(BF)
+            for h in range(4):
+                for e in range(2):
+                    sb[h, c0 + e, slot] = out[e * R : (e + 1) * R, h * HD : (h + 1) * HD]
+
+        project(0, 1)
+        project(1, 2)
+        for e in range(2):
             for d in (2, 1, 3):
-                spread(c, d).start()
-            kept(c).start()
-
-        @pl.when(i == NC)
+                spread(c0 + e, d).start()
+        project(2, 0)
+        for e in range(2):
+            for d in (2, 1, 3):
+                spread_q(c0 + e, d).start()
+            kept(c0 + e).start()
+
+    def share(c):
+        for d in range(4):
+            if d:
+                spread_in(c, d)
+
+            @pl.when(yhi == 0)
+            def _():
+                cross(c, d).start()
+
+            twin(c, d).start()
+
+    def share_far(c):
+        for d in range(4):
+            cross(c, d).wait_recv()
+            twin2(c, d).start()
+
+    def step(i, carry):
+        feed(2 * i)
+
+        @pl.when(i >= 1)
+        def _():
+            projected(2 * i - 2)
+
+        feed(2 * i + 1)
+
+        @pl.when(i >= 1)
+        def _():
+            share(2 * i - 2)
+            share(2 * i - 1)
+
+        @pl.when((i >= 2) & (yhi == 1))
+        def _():
+            share_far(2 * i - 4)
+            share_far(2 * i - 3)
+
+        @pl.when(i == NC // 2)
         def _():
             for r, (sq_, tp_) in enumerate(tp_peers):
                 remote(nall, nrecv.at[r], n_ss.at[r], n_rs.at[r], sq_, tp_).start()
 
-        @pl.when(i == 3)
+        @pl.when(i == 1)
         def _():
             v = csend[0]
             for d in range(3):
@@ -321,25 +368,27 @@
                 v = v + crecv[d]
             csend[1] = v
 
-        @pl.when(i == 4)
+        @pl.when(i == 2)
         def _():
             count_to(1, 3, sibling).start()
 
-        @pl.when(i == 5)
+        @pl.when(i == 3)
         def _():
             count_to(1, 3, sibling).wait_recv()
             csend[2] = csend[1] + crecv[3]
 
-        @pl.when(i == 6)
+        @pl.when(i == 4)
         def _():
             count_to(2, 4, mirror).start()
 
         return carry
 
-    lax.fori_loop(0, NC + 3, step, 0)
+    lax.fori_loop(0, NC // 2 + 1, step, 0)
 
     count_to(2, 4, mirror).wait_recv()
-    counts[...] = csend[2] + crecv[4]
+    csend[3] = csend[2] + crecv[4]
+    told = pltpu.make_async_copy(csend.at[3], counts.at[0], t_sem)
+    told.start()
     ztot = nall[...]
     for r, (sq_, tp_) in enumerate(tp_peers):
         remote(nall, nrecv.at[r], n_ss.at[r], n_rs.at[r], sq_, tp_).wait_recv()
@@ -351,14 +400,10 @@
 
     @pl.when(yhi == 1)
     def _():
-        def tail(c, carry):
-            for d in range(4):
-                cross(c, d).wait_recv()
-                twin2(c, d).start()
-            return carry
-
-        lax.fori_loop(NC - 2, NC, tail, 0)
-
+        share_far(NC - 2)
+        share_far(NC - 1)
+
+    told.wait()
     for r, (sq_, tp_) in enumerate(tp_peers):
         remote(unow, urecv.at[r], u_ss.at[r], u_rs.at[r], sq_, tp_).wait_send()
         remote(nall, nrecv.at[r], n_ss.at[r], n_rs.at[r], sq_, tp_).wait_send()
@@ -373,6 +418,8 @@
         kept(c).wait()
         for d in range(1, 4):
             spread(c, d).wait_send()
+            spread_q(c, d).wait_send()
+            spread_q_in(c, d)
         for d in range(4):
             twin(c, d).wait_send()
             twin_in(c, d).wait_recv()
@@ -396,7 +443,7 @@
 def attention_kernel(att_hbm, cnt_hbm, ctx, att, cnt, vx, m_ref, acc_ref, c_sem, k_sem, v_sem, q_sem):
     seq = lax.axis_index("seq")
     yhi, core = seq // 8, seq % 2
-    counts_in = pltpu.make_async_copy(cnt_hbm, cnt, c_sem)
+    counts_in = pltpu.make_async_copy(cnt_hbm.at[0], cnt, c_sem)
     counts_in.start()
 
     def q_in(qi):
@@ -513,10 +560,10 @@
 
 
 def last_kernel(
-    ctx_hbm, w_hbm,
-    branch,
-    ctx, wbuf, cbuf, snd, snh, own, rcv, rch,
-    c_sem, w_sem, z_ss, z_rs, s_ss, s_rs, h_ss, h_rs,
+    ctx, wbuf, xraw, cols,
+    out,
+    cbuf, snd, snh, own, rcv, rch, kept,
+    z_ss, z_rs, s_ss, s_rs, h_ss, h_rs,
 ):
     seq, tp = where_am_i()
     yhi, z, core = seq // 8, (seq // 2) % 4, seq % 2
@@ -526,11 +573,6 @@
     other_y = x * 2 + 1 - y
     z_peers = [yhi * 8 + ((z + d) % 4) * 2 + core for d in range(1, 4)]
     entered = greet([(p, tp) for p in z_peers] + [(seq, right), (seq, left), (seq, other_y)])
-    ccopy = pltpu.make_async_copy(ctx_hbm, ctx, c_sem)
-    ccopy.start()
-    wcopy = pltpu.make_async_copy(w_hbm, wbuf, w_sem)
-    wcopy.start()
-    ccopy.wait()
     entered()
 
     def back(c, d):
@@ -547,7 +589,6 @@
         for d in (2, 1, 3):
             back(c, d).start()
     cbuf[z] = ctx[z]
-    wcopy.wait()
 
     def pass_on(c, k, to):
         return remote(snd.at[c, k], rcv.at[c, k], s_ss.at[c, k], s_rs.at[c, k], seq, to)
@@ -610,13 +651,22 @@
     lax.fori_loop(0, NO, third, 0)
 
     def fourth(c, carry):
+        rows = pl.ds(pl.multiple_of(c * RO, RO), RO)
+        xv = jnp.swapaxes(xraw[rows], 0, 1)
+        wide = [xv[j].astype(F32) for j in range(S)]
+        for i in range(S):
+            k = 8 + 4 * i
+            v = cols[rows, k : k + 1] * wide[0]
+            for j in range(1, S):
+                v = v + cols[rows, k + j : k + j + 1] * wide[j]
+            kept[i] = v
         pass_on(c, 5, other_y).wait_recv()
+        mine = own[c, 4] + rcv[c, 5].astype(F32)
         pass_on(c, 3, right).wait_recv()
         pass_on(c, 4, left).wait_recv()
-        rows = pl.ds(pl.multiple_of(c * RO, RO), RO)
-        branch[rows, :] = (own[c, 4] + rcv[c, 5].astype(F32)) + (
-            rcv[c, 3].astype(F32) + rcv[c, 4].astype(F32)
-        )
+        branch = mine + (rcv[c, 3].astype(F32) + rcv[c, 4].astype(F32))
+        new = [(kept[i] + cols[rows, 4 + i : 5 + i] * branch).astype(BF) for i in range(S)]
+        out[rows] = jnp.swapaxes(jnp.stack(new, axis=0), 0, 1)
         return carry
 
     lax.fori_loop(0, NO, fourth, 0)
@@ -633,18 +683,15 @@
     lax.fori_loop(0, NO, drain, 0)
 
 
-def combine_kernel(xraw, cols, branch, out):
-    xv = jnp.swapaxes(xraw[...], 0, 1)
-    wide = [xv[j].astype(F32) for j in range(S)]
-    b = branch[...]
-    new = []
-    for i in range(S):
-        v = cols[:, 4 + i : 5 + i] * b
-        for j in range(S):
-            k = 8 + 4 * i + j
-            v = v + cols[:, k : k + 1] * wide[j]
-        new.append(v.astype(BF))
-    out[...] = jnp.swapaxes(jnp.stack(new, axis=0), 0, 1)
+def store_kernel(x, out, sem):
+    copies = [
+        pltpu.make_async_copy(x.at[pl.ds(q * 128, 128)], out.at[pl.ds(q * 128, 128)], sem.at[q])
+        for q in range(4)
+    ]
+    for copy in copies:
+        copy.start()
+    for copy in copies:
+        copy.wait()
 
 
 def local(streams, doc_ids, mix_weight, mix_bias, attn_gain, w_qkv, w_out):
@@ -657,12 +704,12 @@
         first_kernel,
         name="gather_project",
         out_shape=(
-            sds((16, NC, 3, R, HD), BF),
+            sds((BLOCKS, NC, 3, R, HD), BF),
             sds((T, 128), F32),
-            sds((8, 128), jnp.int32),
+            sds((TILES, 8, 128), jnp.int32),
         ),
         in_specs=[hbm] * 6,
-        out_specs=(hbm, vm, vm),
+        out_specs=(hbm, vm, hbm),
         scratch_shapes=[
             VMEM((T, S, W), BF),
             VMEM((S, T, W), BF),
@@ -673,12 +720,13 @@
             VMEM((3, D, W), BF),
             VMEM((NC, 8, R, W), BF),
             VMEM((4, NC, 3, R, HD), BF),
-            VMEM((R, D), BF),
+            VMEM((2 * R, D), BF),
+            VMEM((2 * R, 128), F32),
             VMEM((8, T), F32),
             VMEM((7, 8, T), F32),
             VMEM((24, T), F32),
             VMEM((7, 24, T), F32),
-            VMEM((3, 8, 128), jnp.int32),
+            VMEM((4, 8, 128), jnp.int32),
             VMEM((5, 8, 128), jnp.int32),
             VMEM((T, 128), F32),
             DMA((4,)),
@@ -689,7 +737,9 @@
             DMA((5,)), DMA((5,)),
             DMA((NC, 7)), DMA((NC, 7)),
             DMA((NC, 3)), DMA((NC, 3)),
+            DMA((NC, 3)), DMA((NC, 3)),
             DMA((NC,)),
+            DMA(()),
             DMA((NC, 4)), DMA((NC, 4)),
             DMA((NC, 4)), DMA((NC, 4)),
             DMA((NC, 4)), DMA((NC, 4)),
@@ -713,46 +763,39 @@
             VMEM((T, 128), F32), VMEM((T, 2 * HD), F32),
             DMA(()), DMA((16,)), DMA((16,)), DMA((4,)),
         ],
-        compiler_params=pltpu.CompilerParams(vmem_limit_bytes=60 * 1024 * 1024),
+        compiler_params=pltpu.CompilerParams(vmem_limit_bytes=30 * 1024 * 1024),
     )(att, counts)
-    branch = pl.pallas_call(
+    new = pl.pallas_call(
         last_kernel,
         name="project_out",
-        out_shape=sds((T, W), F32),
-        in_specs=[hbm, hbm],
+        out_shape=sds((T, S, W), BF),
+        in_specs=[vm] * 4,
         out_specs=vm,
         scratch_shapes=[
-            VMEM((4, NO, RO, HD), BF),
-            VMEM((W, D), BF),
             VMEM((4, NO, RO, HD), BF),
             VMEM((NO, 6, RO, W), BF),
             VMEM((NO, 2, RO // 2, W), BF),
             VMEM((NO, 5, RO, W), F32),
             VMEM((NO, 6, RO, W), BF),
             VMEM((NO, 2, RO // 2, W), BF),
-            DMA(()),
-            DMA(()),
+            VMEM((S, RO, W), F32),
             DMA((NO, 3)), DMA((NO, 3)),
             DMA((NO, 6)), DMA((NO, 6)),
             DMA((NO, 2)), DMA((NO, 2)),
         ],
         compiler_params=pltpu.CompilerParams(
-            collective_id=1, has_side_effects=True, vmem_limit_bytes=60 * 1024 * 1024
+            collective_id=1, has_side_effects=True, vmem_limit_bytes=30 * 1024 * 1024
         ),
-    )(ctx, w_out)
+    )(ctx, w_out, streams, mix_cols)
     return pl.pallas_call(
-        combine_kernel,
-        name="combine",
-        grid=(4,),
+        store_kernel,
+        name="store",
         out_shape=sds((T, S, W), BF),
-        in_specs=[
-            pl.BlockSpec((T // 4, S, W), lambda i: (i, 0, 0)),
-            pl.BlockSpec((T // 4, 128), lambda i: (i, 0)),
-            pl.BlockSpec((T // 4, W), lambda i: (i, 0)),
-        ],
-        out_specs=pl.BlockSpec((T // 4, S, W), lambda i: (i, 0, 0)),
-        compiler_params=pltpu.CompilerParams(vmem_limit_bytes=60 * 1024 * 1024),
-    )(streams, mix_cols, branch)
+        in_specs=[vm],
+        out_specs=hbm,
+        scratch_shapes=[DMA((4,))],
+        compiler_params=pltpu.CompilerParams(vmem_limit_bytes=8 * 1024 * 1024),
+    )(new)
 
 
 def solution(mesh):

time: 131 us -> 124 us (0.947)
  the two profiles are of different devices: /device:TPU:16 before, /device:TPU:25 now
where the time goes in v1:
time: 124 us; the launch traced here: 123 us
  Pallas kernels  123 us (99%)
    pallas_call x1, Pallas kernels, local(): pl.pallas_call(first_kernel, name='gather_project', out_shape=(sds((BLOCK...  71.6 us
    pallas_call x1, Pallas kernels, local(): pl.pallas_call(last_kernel, name='project_out', out_shape=sds((T, S, W),...  34.8 us
    pallas_call x1, Pallas kernels, local(): pl.pallas_call(attention_kernel, name='attention', out_shape=sds((4, NO,...  15.6 us

profile of v1, /device:TPU:25, one launch (start us, length us, event | category | flops | bytes accessed | tf_op | source)
XLA Modules:
  0.0 123.4 jit_solution(14231608541264255719)
XLA Ops:
  0.0 71.6 %gather_project.1 = (bf16[160,8,3,64,128]{4,3,2,1,0:T(8,128)(2,1)}, f32[512,128]{1,0:T(8,128)}, s32[9216,8,128]{2,1,0:T(8,128)}) custom-call(bf16[512,4,512]{2,1,0:T(4,128)(2,1)} %xraw.1, s32[4,128]{1,0:T(4,128)} %bitcast.8, f32[4,24,512]{2,1,0:T(8,128)} %bitcast.6, f32[1,24]{1,0:T(1,128)} %bitcast.9, f32[1,4096]{1,0:T(1,128)} %bitcast.7, ...), custom_call_target="tpu_custom_call" | custom-call | tf_op jit(solution)/shard_map/gather_project/pallas_call | solution.py:703
  71.6 0.0 copy-start
  71.6 0.0 copy-start.1
  71.6 0.0 copy-start.2
  71.6 15.6 %attention.1.ctx = bf16[4,4,128,128]{3,2,1,0:T(8,128)(2,1)S(1)} custom-call(bf16[160,8,3,64,128]{4,3,2,1,0:T(8,128)(2,1)} %get-tuple-element.8.att_hbm, s32[9216,8,128]{2,1,0:T(8,128)} %get-tuple-element.9.cnt_hbm), custom_call_target="tpu_custom_call" | custom-call | tf_op jit(solution)/shard_map/attention/pallas_call | solution.py:753
  87.2 0.0 copy-done
  87.2 0.0 copy-done.1
  87.2 0.0 copy-done.2
  87.3 34.8 %project_out.1.x = bf16[512,4,512]{2,1,0:T(4,128)(2,1)S(1)} custom-call(bf16[4,4,128,128]{3,2,1,0:T(8,128)(2,1)S(1)} %attention.1.ctx, bf16[512,4096]{1,0:T(8,128)(2,1)S(1)} %copy-done.1, bf16[512,4,512]{2,1,0:T(4,128)(2,1)S(1)} %copy-done, f32[512,128]{1,0:T(8,128)S(1)} %copy-done.2), custom_call_target="tpu_custom_call" | custom-call | tf_op jit(solution)/shard_map/project_out/pallas_call | solution.py:768
  122.0 1.3 %store.1 = bf16[512,4,512]{2,1,0:T(4,128)(2,1)} custom-call(bf16[512,4,512]{2,1,0:T(4,128)(2,1)S(1)} %project_out.1.x), custom_call_target="tpu_custom_call" | custom-call | tf_op jit(solution)/shard_map/store/pallas_call | solution.py:790
Async XLA Ops:
  71.6 15.6 %copy-start = (bf16[512,4,512]{2,1,0:T(4,128)(2,1)S(1)}, bf16[512,4,512]{2,1,0:T(4,128)(2,1)}, u32[]{:S(2)}) copy-start(bf16[512,4,512]{2,1,0:T(4,128)(2,1)} %xraw.1) | copy-start | bytes 6291460
  71.6 15.6 %copy-start.1 = (bf16[512,4096]{1,0:T(8,128)(2,1)S(1)}, bf16[512,4096]{1,0:T(8,128)(2,1)}, u32[]{:S(2)}) copy-start(bf16[512,4096]{1,0:T(8,128)(2,1)} %wbuf.1) | copy-start | bytes 12582916
  71.6 15.6 %copy-start.2 = (f32[512,128]{1,0:T(8,128)S(1)}, f32[512,128]{1,0:T(8,128)}, u32[]{:S(2)}) copy-start(f32[512,128]{1,0:T(8,128)} %get-tuple-element.10.cols) | copy-start | bytes 786436

commit v2 on v1

--- a/solution.py
+++ b/solution.py
@@ -80,7 +80,7 @@
     att, mix_cols, counts,
     xraw, xs, docs, wmix, bias, gain,
     wbuf, g, sb, gained, norms, unow, urecv, nall, nrecv, csend, crecv, pre_cols,
-    x_sem, i_sem, w_sem, u_ss, u_rs, n_ss, n_rs, c_ss, c_rs, g_ss, g_rs, a_ss, a_rs, q_ss, q_rs, o_sem, t_sem,
+    x_sem, i_sem, w_sem, u_ss, u_rs, n_ss, n_rs, c_ss, c_rs, g_ss, g_rs, a_ss, a_rs, q_rs, o_sem, t_sem,
     sib_ss, sib_rs, x_ss, x_rs, sib2_ss, sib2_rs,
 ):
     seq, tp = where_am_i()
@@ -108,7 +108,7 @@
         small[k].start()
 
     def wcopy(i):
-        return pltpu.make_async_copy(w_hbm.at[i], wbuf.at[i], w_sem.at[i])
+        return pltpu.make_async_copy(w_hbm.at[i], wbuf.at[i], w_sem)
 
     small[0].wait()
     parts = []
@@ -139,12 +139,19 @@
         unow[:, rows] = jnp.where(
             sub < 4, logits[0:8], jnp.where(sub == 4, jnp.broadcast_to(squares, (8, 128)), 0.0)
         )
-        nall[:, rows] = logits[0:24]
+        nall[0, :, rows] = logits[0:24]
 
     entered()
     for r, (sq_, tp_) in enumerate(tp_peers):
-        remote(unow, urecv.at[r], u_ss.at[r], u_rs.at[r], sq_, tp_).start()
-
+        remote(unow, urecv.at[r], u_ss, u_rs, sq_, tp_).start()
+
+    def to_y():
+        return remote(nall.at[0], nrecv.at[0], n_ss.at[0], n_rs.at[0], seq, x * 2 + 1 - y)
+
+    def to_x(k):
+        return remote(nall.at[1], nrecv.at[k], n_ss.at[1], n_rs.at[1], seq, ((x + k) % 4) * 2 + y)
+
+    to_y().start()
     for k in range(1, 4):
         small[k].wait()
     dv = docs[...]
@@ -158,11 +165,11 @@
     bias_col = jnp.sum(jnp.where(diag, jnp.broadcast_to(bias[...], (24, 24)), 0.0), axis=1, keepdims=True)
 
     def count_to(level, k, to):
-        return remote(csend.at[level], crecv.at[k], c_ss.at[k], c_rs.at[k], to, tp)
+        return remote(csend.at[level], crecv.at[k], c_ss, c_rs.at[level], to, tp)
 
     total = unow[...]
-    for r, (sq_, tp_) in enumerate(tp_peers):
-        remote(unow, urecv.at[r], u_ss.at[r], u_rs.at[r], sq_, tp_).wait_recv()
+    remote(urecv, urecv, u_ss, u_rs, seq, tp_peers[0][1]).wait_recv()
+    for r in range(7):
         total = total + urecv[r]
     inv_rms = lax.rsqrt(total[4:5] / (S * D) + EPS)
     pre = 1.0 / (1.0 + jnp.exp(-(total * inv_rms + bias_col[0:8])))
@@ -172,15 +179,15 @@
     left = ((x + 3) % 4) * 2 + y
     other_y = x * 2 + 1 - y
     b_p = other_y
-    b_l0, b_l1 = left, ((x + 3) % 4) * 2 + 1 - y
-    b_r0, b_r1 = right, ((x + 1) % 4) * 2 + 1 - y
-    b_f0, b_f1 = ((x + 2) % 4) * 2 + y, ((x + 2) % 4) * 2 + 1 - y
-
-    def move(c, k, blk, role, to):
-        return remote(g.at[c, blk], g.at[c, blk], g_ss.at[c, k], g_rs.at[c, role], seq, to)
-
-    def arrived(c, role, blk):
-        move(c, 0, blk, role, right).wait_recv()
+    b_l0 = left
+    b_r1 = ((x + 1) % 4) * 2 + 1 - y
+
+    def move(c, blk, role, to):
+        return remote(g.at[c, blk], g.at[c, blk], g_ss, g_rs.at[c, role], seq, to)
+
+    def arrived(c, role, n):
+        some = g.at[c, pl.ds(0, n)]
+        remote(some, some, g_ss, g_rs.at[c, role], seq, right).wait_recv()
 
     def make_chunk(c):
         rows = slice(c * R, (c + 1) * R)
@@ -190,9 +197,9 @@
         g[c, tp] = v.astype(BF)
 
     def send_chunk(c):
-        move(c, 2, tp, 0, other_y).start()
-        move(c, 0, tp, 1, right).start()
-        move(c, 1, tp, 3, left).start()
+        move(c, tp, 0, other_y).start()
+        move(c, tp, 1, right).start()
+        move(c, tp, 3, left).start()
 
     make_chunk(0)
     for c in range(NC):
@@ -202,8 +209,7 @@
             send_chunk(c)
     for d in range(3):
         count_to(0, d, z_peers[d]).start()
-    for i in range(3):
-        wcopy(i).wait()
+    pltpu.make_async_copy(w_hbm, wbuf, w_sem).wait()
 
     def block_of(half, d):
         return half * 8 + ((z + 4 - d) % 4) * 2 + core
@@ -213,57 +219,41 @@
     def spread(c, d):
         return remote(
             sb.at[(z + d) % 4, c, two], att.at[seq, c, two],
-            a_ss.at[c, d - 1], a_rs.at[c, d - 1], z_peers[d - 1], tp,
+            a_ss, a_rs.at[c], z_peers[d - 1], tp,
         )
 
-    def spread_in(c, d):
-        remote(
-            sb.at[z, c, two], att.at[block_of(yhi, d), c, two],
-            a_ss.at[c, d - 1], a_rs.at[c, d - 1], z_peers[d - 1], tp,
-        ).wait_recv()
+    def spread_in(c):
+        ref = sb.at[pl.ds(0, 3), c, two]
+        remote(ref, ref, a_ss, a_rs.at[c], z_peers[0], tp).wait_recv()
 
     def spread_q(c, d):
         return remote(
             sb.at[(z + d) % 4, c, 2], att.at[seq, c, 2],
-            q_ss.at[c, d - 1], q_rs.at[c, d - 1], z_peers[d - 1], tp,
+            a_ss, q_rs, z_peers[d - 1], tp,
         )
 
-    def spread_q_in(c, d):
-        remote(
-            sb.at[z, c, 2], att.at[block_of(yhi, d), c, 2],
-            q_ss.at[c, d - 1], q_rs.at[c, d - 1], z_peers[d - 1], tp,
-        ).wait_recv()
-
-    def kept(c):
-        return pltpu.make_async_copy(sb.at[z, c], att.at[seq, c], o_sem.at[c])
+    def kept():
+        return pltpu.make_async_copy(sb.at[z], att.at[seq], o_sem)
 
     def kv(c, d):
         return sb.at[z, c, pl.ds(0, 2)] if d == 0 else att.at[block_of(yhi, d), c, pl.ds(0, 2)]
 
     def twin(c, d):
         dst = att.at[block_of(yhi, d), c, pl.ds(0, 2)]
-        return remote(kv(c, d), dst, sib_ss.at[c, d], sib_rs.at[c, d], sibling, tp)
-
-    def twin_in(c, d):
-        dst = att.at[yhi * 8 + ((z + 4 - d) % 4) * 2 + 1 - core, c, pl.ds(0, 2)]
-        return remote(kv(c, d), dst, sib_ss.at[c, d], sib_rs.at[c, d], sibling, tp)
+        return remote(kv(c, d), dst, sib_ss, sib_rs, sibling, tp)
 
     def cross(c, d):
         dst = att.at[block_of(0, d), c, pl.ds(0, 2)]
-        return remote(kv(c, d), dst, x_ss.at[c, d], x_rs.at[c, d], mirror, tp)
+        return remote(kv(c, d), dst, x_ss, x_rs.at[c], mirror, tp)
 
     def twin2(c, d):
         ref = att.at[block_of(0, d), c, pl.ds(0, 2)]
-        return remote(ref, ref, sib2_ss.at[c, d], sib2_rs.at[c, d], sibling, tp)
-
-    def twin2_in(c, d):
-        dst = att.at[((z + 4 - d) % 4) * 2 + 1 - core, c, pl.ds(0, 2)]
-        return remote(dst, dst, sib2_ss.at[c, d], sib2_rs.at[c, d], sibling, tp)
+        return remote(ref, ref, sib2_ss, sib2_rs, sibling, tp)
 
     def hand_on(i):
-        arrived(i, 0, b_p)
-        move(i, 3, b_p, 2, right).start()
-        move(i, 4, b_p, 4, left).start()
+        arrived(i, 0, 1)
+        move(i, b_p, 3, right).start()
+        move(i, b_p, 2, left).start()
 
     hand_on(0)
 
@@ -278,19 +268,16 @@
 
         @pl.when(i < NC)
         def _():
-            arrived(i, 1, b_l0)
-            move(i, 5, b_l0, 5, right).start()
-            arrived(i, 4, b_r1)
-            move(i, 6, b_r1, 6, left).start()
+            arrived(i, 1, 1)
+            move(i, b_l0, 3, right).start()
+            arrived(i, 2, 1)
+            move(i, b_r1, 3, left).start()
 
     def projected(c0):
         for e in range(2):
             c = c0 + e
             rows = slice(e * R, (e + 1) * R)
-            arrived(c, 2, b_l1)
-            arrived(c, 3, b_r0)
-            arrived(c, 5, b_f0)
-            arrived(c, 6, b_f1)
+            arrived(c, 3, 4)
             ss = jnp.zeros((R, 128), F32)
             for b in range(8):
                 g32 = g[c, b].astype(F32)
@@ -318,12 +305,10 @@
         for e in range(2):
             for d in (2, 1, 3):
                 spread_q(c0 + e, d).start()
-            kept(c0 + e).start()
 
     def share(c):
+        spread_in(c)
         for d in range(4):
-            if d:
-                spread_in(c, d)
 
             @pl.when(yhi == 0)
             def _():
@@ -332,8 +317,9 @@
             twin(c, d).start()
 
     def share_far(c):
+        ref = sb.at[:, c, two]
+        remote(ref, ref, x_ss, x_rs.at[c], mirror, tp).wait_recv()
         for d in range(4):
-            cross(c, d).wait_recv()
             twin2(c, d).start()
 
     def step(i, carry):
@@ -355,16 +341,18 @@
             share_far(2 * i - 4)
             share_far(2 * i - 3)
 
-        @pl.when(i == NC // 2)
-        def _():
-            for r, (sq_, tp_) in enumerate(tp_peers):
-                remote(nall, nrecv.at[r], n_ss.at[r], n_rs.at[r], sq_, tp_).start()
+        @pl.when(i == NC // 2 - 1)
+        def _():
+            for k in (2, 1, 3):
+                to_x(k).start()
 
         @pl.when(i == 1)
         def _():
+            to_y().wait_recv()
+            nall[1] = nall[0] + nrecv[0]
             v = csend[0]
+            remote(crecv.at[pl.ds(0, 3)], crecv.at[pl.ds(0, 3)], c_ss, c_rs.at[0], sibling, tp).wait_recv()
             for d in range(3):
-                count_to(0, d, z_peers[d]).wait_recv()
                 v = v + crecv[d]
             csend[1] = v
 
@@ -384,15 +372,15 @@
         return carry
 
     lax.fori_loop(0, NC // 2 + 1, step, 0)
+    kept().start()
 
     count_to(2, 4, mirror).wait_recv()
     csend[3] = csend[2] + crecv[4]
     told = pltpu.make_async_copy(csend.at[3], counts.at[0], t_sem)
     told.start()
-    ztot = nall[...]
-    for r, (sq_, tp_) in enumerate(tp_peers):
-        remote(nall, nrecv.at[r], n_ss.at[r], n_rs.at[r], sq_, tp_).wait_recv()
-        ztot = ztot + nrecv[r]
+    three = nrecv.at[pl.ds(1, 3)]
+    remote(three, three, n_ss.at[1], n_rs.at[1], seq, right).wait_recv()
+    ztot = (nall[1] + nrecv[1]) + (nrecv[2] + nrecv[3])
     ztot = ztot * inv_rms + bias_col
     post = 2.0 / (1.0 + jnp.exp(-ztot[0:8]))
     e0, e1 = balanced(jnp.exp(ztot[8:16]), jnp.exp(ztot[16:24]))
@@ -404,40 +392,31 @@
         share_far(NC - 1)
 
     told.wait()
-    for r, (sq_, tp_) in enumerate(tp_peers):
-        remote(unow, urecv.at[r], u_ss.at[r], u_rs.at[r], sq_, tp_).wait_send()
-        remote(nall, nrecv.at[r], n_ss.at[r], n_rs.at[r], sq_, tp_).wait_send()
-    for d in range(3):
-        count_to(0, d, z_peers[d]).wait_send()
-    count_to(1, 3, sibling).wait_send()
-    count_to(2, 4, mirror).wait_send()
-
-    def drain(c, carry):
-        for k in range(7):
-            move(c, k, tp, 0, right).wait_send()
-        kept(c).wait()
-        for d in range(1, 4):
-            spread(c, d).wait_send()
-            spread_q(c, d).wait_send()
-            spread_q_in(c, d)
-        for d in range(4):
-            twin(c, d).wait_send()
-            twin_in(c, d).wait_recv()
-
-        @pl.when(yhi == 0)
-        def _():
-            for d in range(4):
-                cross(c, d).wait_send()
-
-        @pl.when(yhi == 1)
-        def _():
-            for d in range(4):
-                twin2(c, d).wait_send()
-                twin2_in(c, d).wait_recv()
-
-        return carry
-
-    lax.fori_loop(0, NC, drain, 0)
+    kept().wait()
+
+    def all_of(ref, ssem, rsem):
+        return remote(ref, ref, ssem, rsem, sibling, tp)
+
+    all_of(urecv, u_ss, u_rs).wait_send()
+    all_of(nall.at[0], n_ss.at[0], n_rs.at[0]).wait_send()
+    all_of(three, n_ss.at[1], n_rs.at[1]).wait_send()
+    all_of(crecv, c_ss, c_rs.at[0]).wait_send()
+    all_of(g.at[pl.ds(0, 7)], g_ss, g_rs.at[0, 0]).wait_send()
+    all_of(sb.at[pl.ds(0, 3)], a_ss, a_rs.at[0]).wait_send()
+    all_of(sb.at[pl.ds(0, 3), :, 2], a_ss, q_rs).wait_recv()
+    twins = all_of(sb.at[:, :, two], sib_ss, sib_rs)
+    twins.wait_send()
+    twins.wait_recv()
+
+    @pl.when(yhi == 0)
+    def _():
+        all_of(sb.at[:, :, two], x_ss, x_rs.at[0]).wait_send()
+
+    @pl.when(yhi == 1)
+    def _():
+        far = all_of(sb.at[:, :, two], sib2_ss, sib2_rs)
+        far.wait_send()
+        far.wait_recv()
 
 
 def attention_kernel(att_hbm, cnt_hbm, ctx, att, cnt, vx, m_ref, acc_ref, c_sem, k_sem, v_sem, q_sem):
@@ -457,6 +436,8 @@
         return pltpu.make_async_copy(att_hbm.at[kb, :, 1], vx.at[kb, :, :, pl.ds(0, HD)], v_sem.at[kb])
 
     q_in(0).start()
+    k_in(yhi * 8 + core).start()
+    v_in(yhi * 8 + core).start()
     counts_in.wait()
     starts = [cnt[k, 0] for k in range(1, 4)]
     scale = HD ** (-0.5) * 1.4426950408889634
@@ -479,7 +460,7 @@
         v_in(kb).wait()
         return c
 
-    lax.fori_loop(first_needed, yhi * 8 + core + 1, fetch, 0)
+    lax.fori_loop(first_needed, yhi * 8 + core, fetch, 0)
     for qi in range(1, 4):
         q_in(qi).start()
     lax.fori_loop(yhi * 8 + core + 1, yhi * 8 + core + 7, fetch, 0)
@@ -492,8 +473,8 @@
 
     def one_query_block(qi, carry):
         qb = yhi * 8 + qi * 2 + core
-        lax.fori_loop(jnp.where(qi == 0, first_needed, qb - 1), qb + 1, land, 0)
         q_in(qi).wait()
+        land(qb, 0)
         q = att[qb, :, 2].reshape(T, HD)
         first = start_of(qb * T)
         last = start_of(qb * T + T - 1)
@@ -548,6 +529,7 @@
             return c
 
         block(qb, "diagonal")
+        lax.fori_loop(jnp.where(qi == 0, first_needed, qb - 1), qb, land, 0)
         lax.fori_loop(lo, mid, some, 0)
         pairs = (qb - mid) // 2
         lax.fori_loop(0, pairs, two, 0)
@@ -577,13 +559,12 @@
 
     def back(c, d):
         return remote(
-            ctx.at[(z + d) % 4, c], cbuf.at[z, c], z_ss.at[c, d - 1], z_rs.at[c, d - 1], z_peers[d - 1], tp
+            ctx.at[(z + d) % 4, c], cbuf.at[z, c], z_ss, z_rs.at[c], z_peers[d - 1], tp
         )
 
-    def back_in(c, d):
-        remote(
-            ctx.at[z, c], cbuf.at[(z + 4 - d) % 4, c], z_ss.at[c, d - 1], z_rs.at[c, d - 1], z_peers[d - 1], tp
-        ).wait_recv()
+    def back_in(c):
+        ref = ctx.at[pl.ds(0, 3), c]
+        remote(ref, ref, z_ss, z_rs.at[c], z_peers[0], tp).wait_recv()
 
     for c in range(NO):
         for d in (2, 1, 3):
@@ -591,16 +572,15 @@
     cbuf[z] = ctx[z]
 
     def pass_on(c, k, to):
-        return remote(snd.at[c, k], rcv.at[c, k], s_ss.at[c, k], s_rs.at[c, k], seq, to)
+        return remote(snd.at[c, k], rcv.at[c, k], s_ss, s_rs.at[c, k], seq, to)
 
     def half(c, k, to):
-        return remote(snh.at[c, k], rch.at[c, k], h_ss.at[c, k], h_rs.at[c, k], seq, to)
+        return remote(snh.at[c, k], rch.at[c, k], h_ss, h_rs.at[c, k], seq, to)
 
     to_right, to_left, far = ((x + 1) % 4) * 2, ((x + 3) % 4) * 2, ((x + 2) % 4) * 2
 
     def project(c, carry):
-        for d in range(1, 4):
-            back_in(c, d)
+        back_in(c)
         lhs = jnp.concatenate([cbuf[h, c] for h in range(4)], axis=1)
 
         def term(b):
@@ -671,16 +651,10 @@
 
     lax.fori_loop(0, NO, fourth, 0)
 
-    def drain(c, carry):
-        for d in range(1, 4):
-            back(c, d).wait_send()
-        for k in range(6):
-            pass_on(c, k, right).wait_send()
-        half(c, 0, right).wait_send()
-        half(c, 1, left).wait_send()
-        return carry
-
-    lax.fori_loop(0, NO, drain, 0)
+    everything = ctx.at[pl.ds(0, 3)]
+    remote(everything, everything, z_ss, z_rs.at[0], seq, right).wait_send()
+    remote(snd, snd, s_ss, s_rs.at[0, 0], seq, right).wait_send()
+    remote(snh, snh, h_ss, h_rs.at[0, 0], seq, right).wait_send()
 
 
 def store_kernel(x, out, sem):
@@ -724,25 +698,25 @@
             VMEM((2 * R, 128), F32),
             VMEM((8, T), F32),
             VMEM((7, 8, T), F32),
-            VMEM((24, T), F32),
-            VMEM((7, 24, T), F32),
+            VMEM((2, 24, T), F32),
+            VMEM((4, 24, T), F32),
             VMEM((4, 8, 128), jnp.int32),
             VMEM((5, 8, 128), jnp.int32),
             VMEM((T, 128), F32),
             DMA((4,)),
             DMA((4,)),
-            DMA((3,)),
-            DMA((7,)), DMA((7,)),
-            DMA((7,)), DMA((7,)),
-            DMA((5,)), DMA((5,)),
-            DMA((NC, 7)), DMA((NC, 7)),
-            DMA((NC, 3)), DMA((NC, 3)),
-            DMA((NC, 3)), DMA((NC, 3)),
-            DMA((NC,)),
             DMA(()),
-            DMA((NC, 4)), DMA((NC, 4)),
-            DMA((NC, 4)), DMA((NC, 4)),
-            DMA((NC, 4)), DMA((NC, 4)),
+            DMA(()), DMA(()),
+            DMA((2,)), DMA((2,)),
+            DMA(()), DMA((3,)),
+            DMA(()), DMA((NC, 4)),
+            DMA(()), DMA((NC,)),
+            DMA(()),
+            DMA(()),
+            DMA(()),
+            DMA(()), DMA(()),
+            DMA(()), DMA((NC,)),
+            DMA(()), DMA(()),
         ],
         compiler_params=pltpu.CompilerParams(
             collective_id=0, has_side_effects=True, vmem_limit_bytes=60 * 1024 * 1024
@@ -779,9 +753,9 @@
             VMEM((NO, 6, RO, W), BF),
             VMEM((NO, 2, RO // 2, W), BF),
             VMEM((S, RO, W), F32),
-            DMA((NO, 3)), DMA((NO, 3)),
-            DMA((NO, 6)), DMA((NO, 6)),
-            DMA((NO, 2)), DMA((NO, 2)),
+            DMA(()), DMA((NO,)),
+            DMA(()), DMA((NO, 6)),
+            DMA(()), DMA((NO, 2)),
         ],
         compiler_params=pltpu.CompilerParams(
             collective_id=1, has_side_effects=True, vmem_limit_bytes=30 * 1024 * 1024

time: 124 us -> 118 us (0.952)
  Pallas kernels: 123 us -> 117 us
    pallas_call x1, Pallas kernels: 71.6 us -> 65.4 us  [local(): pl.pallas_call(first_kernel, name='gather_project', out_shape=(sds((BLOCK...]
    pallas_call x1, Pallas kernels: 15.6 us -> 18.2 us  [local(): pl.pallas_call(attention_kernel, name='attention', out_shape=sds((4, NO,...]
    pallas_call x1, Pallas kernels: 34.8 us -> 32.3 us  [local(): pl.pallas_call(last_kernel, name='project_out', out_shape=sds((T, S, W),...]
where the time goes in v2:
time: 118 us; the launch traced here: 117 us
  Pallas kernels  117 us (99%)
    pallas_call x1, Pallas kernels, local(): pl.pallas_call(first_kernel, name='gather_project', out_shape=(sds((BLOCK...  65.4 us
    pallas_call x1, Pallas kernels, local(): pl.pallas_call(last_kernel, name='project_out', out_shape=sds((T, S, W),...  32.3 us
    pallas_call x1, Pallas kernels, local(): pl.pallas_call(attention_kernel, name='attention', out_shape=sds((4, NO,...  18.2 us

profile of v2, /device:TPU:25, one launch (start us, length us, event | category | flops | bytes accessed | tf_op | source)
XLA Modules:
  0.0 117.3 jit_solution(1312857104702184872)
XLA Ops:
  0.0 65.4 %gather_project.1 = (bf16[160,8,3,64,128]{4,3,2,1,0:T(8,128)(2,1)}, f32[512,128]{1,0:T(8,128)}, s32[9216,8,128]{2,1,0:T(8,128)}) custom-call(bf16[512,4,512]{2,1,0:T(4,128)(2,1)} %xraw.1, s32[4,128]{1,0:T(4,128)} %bitcast.8, f32[4,24,512]{2,1,0:T(8,128)} %bitcast.6, f32[1,24]{1,0:T(1,128)} %bitcast.9, f32[1,4096]{1,0:T(1,128)} %bitcast.7, ...), custom_call_target="tpu_custom_call" | custom-call | tf_op jit(solution)/shard_map/gather_project/pallas_call | solution.py:677
  65.4 0.0 copy-start
  65.4 0.0 copy-start.1
  65.4 0.0 copy-start.2
  65.4 18.2 %attention.1.ctx = bf16[4,4,128,128]{3,2,1,0:T(8,128)(2,1)S(1)} custom-call(bf16[160,8,3,64,128]{4,3,2,1,0:T(8,128)(2,1)} %get-tuple-element.8.att_hbm, s32[9216,8,128]{2,1,0:T(8,128)} %get-tuple-element.9.cnt_hbm), custom_call_target="tpu_custom_call" | custom-call | tf_op jit(solution)/shard_map/attention/pallas_call | solution.py:727
  83.7 0.0 copy-done
  83.7 0.0 copy-done.1
  83.7 0.0 copy-done.2
  83.7 32.3 %project_out.1.x = bf16[512,4,512]{2,1,0:T(4,128)(2,1)S(1)} custom-call(bf16[4,4,128,128]{3,2,1,0:T(8,128)(2,1)S(1)} %attention.1.ctx, bf16[512,4096]{1,0:T(8,128)(2,1)S(1)} %copy-done.1, bf16[512,4,512]{2,1,0:T(4,128)(2,1)S(1)} %copy-done, f32[512,128]{1,0:T(8,128)S(1)} %copy-done.2), custom_call_target="tpu_custom_call" | custom-call | tf_op jit(solution)/shard_map/project_out/pallas_call | solution.py:742
  116.0 1.3 %store.1 = bf16[512,4,512]{2,1,0:T(4,128)(2,1)} custom-call(bf16[512,4,512]{2,1,0:T(4,128)(2,1)S(1)} %project_out.1.x), custom_call_target="tpu_custom_call" | custom-call | tf_op jit(solution)/shard_map/store/pallas_call | solution.py:764
Async XLA Ops:
  65.4 18.3 %copy-start = (bf16[512,4,512]{2,1,0:T(4,128)(2,1)S(1)}, bf16[512,4,512]{2,1,0:T(4,128)(2,1)}, u32[]{:S(2)}) copy-start(bf16[512,4,512]{2,1,0:T(4,128)(2,1)} %xraw.1) | copy-start | bytes 6291460
  65.4 18.3 %copy-start.1 = (bf16[512,4096]{1,0:T(8,128)(2,1)S(1)}, bf16[512,4096]{1,0:T(8,128)(2,1)}, u32[]{:S(2)}) copy-start(bf16[512,4096]{1,0:T(8,128)(2,1)} %wbuf.1) | copy-start | bytes 12582916
  65.4 18.3 %copy-start.2 = (f32[512,128]{1,0:T(8,128)S(1)}, f32[512,128]{1,0:T(8,128)}, u32[]{:S(2)}) copy-start(f32[512,128]{1,0:T(8,128)} %get-tuple-element.10.cols) | copy-start | bytes 786436

commit v3 on v2

--- a/solution.py
+++ b/solution.py
@@ -18,7 +18,8 @@
 BLOCKS = 160
 TILES = 9216
 HALF = 256
-AHEAD = 3
+AHEAD = 4
+HANDED = 2
 R = T // NC
 F32 = jnp.float32
 BF = jnp.bfloat16
@@ -87,7 +88,8 @@
     yhi, z, core = seq // 8, (seq // 2) % 4, seq % 2
     x, y = tp // 2, tp % 2
     sibling, mirror = seq + 1 - 2 * core, (seq + 8) % 16
-    tp_peers = [(seq, (tp + r) % 8) for r in range(1, 8)]
+    far_first = ((2, 1), (2, 0), (1, 1), (3, 1), (1, 0), (3, 0), (0, 1))
+    tp_peers = [(seq, ((x + dx) % 4) * 2 + (y + dy) % 2) for dx, dy in far_first]
     z_peers = [yhi * 8 + ((z + d) % 4) * 2 + core for d in range(1, 4)]
     entered = greet(tp_peers + [(p, tp) for p in z_peers] + [(sibling, tp), (mirror, tp)])
 
@@ -179,8 +181,11 @@
     left = ((x + 3) % 4) * 2 + y
     other_y = x * 2 + 1 - y
     b_p = other_y
-    b_l0 = left
-    b_r1 = ((x + 1) % 4) * 2 + 1 - y
+    b_far = ((x + 2) % 4) * 2 + y
+
+    def half_on(c, h, to):
+        rows = g.at[c, right if h else left, pl.ds(h * (R // 2), R // 2)]
+        return remote(rows, rows, g_ss, g_rs.at[c, 2], seq, to)
 
     def move(c, blk, role, to):
         return remote(g.at[c, blk], g.at[c, blk], g_ss, g_rs.at[c, role], seq, to)
@@ -199,7 +204,7 @@
     def send_chunk(c):
         move(c, tp, 0, other_y).start()
         move(c, tp, 1, right).start()
-        move(c, tp, 3, left).start()
+        move(c, tp, 1, left).start()
 
     make_chunk(0)
     for c in range(NC):
@@ -253,31 +258,36 @@
     def hand_on(i):
         arrived(i, 0, 1)
         move(i, b_p, 3, right).start()
-        move(i, b_p, 2, left).start()
-
-    hand_on(0)
+        move(i, b_p, 3, left).start()
+
+    for c in range(HANDED):
+        hand_on(c)
 
     def feed(i):
         @pl.when(i + AHEAD < NC)
         def _():
             send_chunk(i + AHEAD)
 
-        @pl.when(i + 1 < NC)
-        def _():
-            hand_on(i + 1)
+        @pl.when(i + HANDED < NC)
+        def _():
+            hand_on(i + HANDED)
 
         @pl.when(i < NC)
         def _():
-            arrived(i, 1, 1)
-            move(i, b_l0, 3, right).start()
-            arrived(i, 2, 1)
-            move(i, b_r1, 3, left).start()
+            arrived(i, 1, 2)
+            half_on(i, 0, right).start()
+            half_on(i, 1, left).start()
+
+        @pl.when((i >= 1) & (i <= NC))
+        def _():
+            arrived(i - 1, 2, 1)
+            move(i - 1, b_far, 3, other_y).start()
 
     def projected(c0):
         for e in range(2):
             c = c0 + e
             rows = slice(e * R, (e + 1) * R)
-            arrived(c, 3, 4)
+            arrived(c, 3, 3)
             ss = jnp.zeros((R, 128), F32)
             for b in range(8):
                 g32 = g[c, b].astype(F32)
@@ -323,6 +333,14 @@
             twin2(c, d).start()
 
     def step(i, carry):
+        @pl.when(i == 1)
+        def _():
+            count_to(1, 3, sibling).start()
+
+        @pl.when(i == 2)
+        def _():
+            count_to(2, 4, mirror).start()
+
         feed(2 * i)
 
         @pl.when(i >= 1)
@@ -331,22 +349,7 @@
 
         feed(2 * i + 1)
 
-        @pl.when(i >= 1)
-        def _():
-            share(2 * i - 2)
-            share(2 * i - 1)
-
-        @pl.when((i >= 2) & (yhi == 1))
-        def _():
-            share_far(2 * i - 4)
-            share_far(2 * i - 3)
-
-        @pl.when(i == NC // 2 - 1)
-        def _():
-            for k in (2, 1, 3):
-                to_x(k).start()
-
-        @pl.when(i == 1)
+        @pl.when(i == 0)
         def _():
             to_y().wait_recv()
             nall[1] = nall[0] + nrecv[0]
@@ -356,18 +359,25 @@
                 v = v + crecv[d]
             csend[1] = v
 
-        @pl.when(i == 2)
-        def _():
-            count_to(1, 3, sibling).start()
-
-        @pl.when(i == 3)
+        @pl.when(i == 1)
         def _():
             count_to(1, 3, sibling).wait_recv()
             csend[2] = csend[1] + crecv[3]
 
-        @pl.when(i == 4)
-        def _():
-            count_to(2, 4, mirror).start()
+        @pl.when(i >= 1)
+        def _():
+            share(2 * i - 2)
+            share(2 * i - 1)
+
+        @pl.when((i >= 2) & (yhi == 1))
+        def _():
+            share_far(2 * i - 4)
+            share_far(2 * i - 3)
+
+        @pl.when(i == NC // 2 - 1)
+        def _():
+            for k in (2, 1, 3):
+                to_x(k).start()
 
         return carry
 

time: 118 us -> 134 us (1.14)
  Pallas kernels: 117 us -> 132 us
    pallas_call x1, Pallas kernels: 65.4 us -> 80.2 us  [local(): pl.pallas_call(first_kernel, name='gather_project', out_shape=(sds((BLOCK...]
    pallas_call x1, Pallas kernels: 32.3 us -> 35.8 us  [local(): pl.pallas_call(last_kernel, name='project_out', out_shape=sds((T, S, W),...]
    pallas_call x1, Pallas kernels: 18.2 us -> 14.9 us  [local(): pl.pallas_call(attention_kernel, name='attention', out_shape=sds((4, NO,...]
where the time goes in v3:
time: 134 us; the launch traced here: 132 us
  Pallas kernels  132 us (99%)
    pallas_call x1, Pallas kernels, local(): pl.pallas_call(first_kernel, name='gather_project', out_shape=(sds((BLOCK...  80.2 us
    pallas_call x1, Pallas kernels, local(): pl.pallas_call(last_kernel, name='project_out', out_shape=sds((T, S, W),...  35.8 us
    pallas_call x1, Pallas kernels, local(): pl.pallas_call(attention_kernel, name='attention', out_shape=sds((4, NO,...  14.9 us

profile of v3, /device:TPU:25, one launch (start us, length us, event | category | flops | bytes accessed | tf_op | source)
XLA Modules:
  0.0 132.2 jit_solution(15318617165649992649)
XLA Ops:
  0.0 80.2 %gather_project.1 = (bf16[160,8,3,64,128]{4,3,2,1,0:T(8,128)(2,1)}, f32[512,128]{1,0:T(8,128)}, s32[9216,8,128]{2,1,0:T(8,128)}) custom-call(bf16[512,4,512]{2,1,0:T(4,128)(2,1)} %xraw.1, s32[4,128]{1,0:T(4,128)} %bitcast.8, f32[4,24,512]{2,1,0:T(8,128)} %bitcast.6, f32[1,24]{1,0:T(1,128)} %bitcast.9, f32[1,4096]{1,0:T(1,128)} %bitcast.7, ...), custom_call_target="tpu_custom_call" | custom-call | tf_op jit(solution)/shard_map/gather_project/pallas_call | solution.py:687
  80.2 0.0 copy-start
  80.2 0.0 copy-start.1
  80.2 0.0 copy-start.2
  80.2 14.9 %attention.1.ctx = bf16[4,4,128,128]{3,2,1,0:T(8,128)(2,1)S(1)} custom-call(bf16[160,8,3,64,128]{4,3,2,1,0:T(8,128)(2,1)} %get-tuple-element.8.att_hbm, s32[9216,8,128]{2,1,0:T(8,128)} %get-tuple-element.9.cnt_hbm), custom_call_target="tpu_custom_call" | custom-call | tf_op jit(solution)/shard_map/attention/pallas_call | solution.py:737
  95.1 0.0 copy-done
  95.1 0.0 copy-done.1
  95.1 0.0 copy-done.2
  95.1 35.8 %project_out.1.x = bf16[512,4,512]{2,1,0:T(4,128)(2,1)S(1)} custom-call(bf16[4,4,128,128]{3,2,1,0:T(8,128)(2,1)S(1)} %attention.1.ctx, bf16[512,4096]{1,0:T(8,128)(2,1)S(1)} %copy-done.1, bf16[512,4,512]{2,1,0:T(4,128)(2,1)S(1)} %copy-done, f32[512,128]{1,0:T(8,128)S(1)} %copy-done.2), custom_call_target="tpu_custom_call" | custom-call | tf_op jit(solution)/shard_map/project_out/pallas_call | solution.py:752
  130.9 1.3 %store.1 = bf16[512,4,512]{2,1,0:T(4,128)(2,1)} custom-call(bf16[512,4,512]{2,1,0:T(4,128)(2,1)S(1)} %project_out.1.x), custom_call_target="tpu_custom_call" | custom-call | tf_op jit(solution)/shard_map/store/pallas_call | solution.py:774
Async XLA Ops:
  80.2 14.9 %copy-start = (bf16[512,4,512]{2,1,0:T(4,128)(2,1)S(1)}, bf16[512,4,512]{2,1,0:T(4,128)(2,1)}, u32[]{:S(2)}) copy-start(bf16[512,4,512]{2,1,0:T(4,128)(2,1)} %xraw.1) | copy-start | bytes 6291460
  80.2 14.9 %copy-start.1 = (bf16[512,4096]{1,0:T(8,128)(2,1)S(1)}, bf16[512,4096]{1,0:T(8,128)(2,1)}, u32[]{:S(2)}) copy-start(bf16[512,4096]{1,0:T(8,128)(2,1)} %wbuf.1) | copy-start | bytes 12582916
  80.2 14.9 %copy-start.2 = (f32[512,128]{1,0:T(8,128)S(1)}, f32[512,128]{1,0:T(8,128)}, u32[]{:S(2)}) copy-start(f32[512,128]{1,0:T(8,128)} %get-tuple-element.10.cols) | copy-start | bytes 786436

commit v4 on v3

--- a/solution.py
+++ b/solution.py
@@ -18,8 +18,8 @@
 BLOCKS = 160
 TILES = 9216
 HALF = 256
-AHEAD = 4
-HANDED = 2
+AHEAD = 3
+HANDED = 1
 R = T // NC
 F32 = jnp.float32
 BF = jnp.bfloat16
@@ -80,8 +80,8 @@
     x_hbm, docs_hbm, wmix_hbm, bias_hbm, gain_hbm, w_hbm,
     att, mix_cols, counts,
     xraw, xs, docs, wmix, bias, gain,
-    wbuf, g, sb, gained, norms, unow, urecv, nall, nrecv, csend, crecv, pre_cols,
-    x_sem, i_sem, w_sem, u_ss, u_rs, n_ss, n_rs, c_ss, c_rs, g_ss, g_rs, a_ss, a_rs, q_rs, o_sem, t_sem,
+    wbuf, g, sb, gained, norms, unow, urecv, nall, nrecv, csend, crecv, pre_cols, cols,
+    x_sem, i_sem, w_sem, u_ss, u_rs, n_ss, n_rs, c_ss, c_rs, g_ss, g_rs, a_ss, a_rs, q_rs, o_sem, t_sem, m_sem,
     sib_ss, sib_rs, x_ss, x_rs, sib2_ss, sib2_rs,
 ):
     seq, tp = where_am_i()
@@ -181,11 +181,8 @@
     left = ((x + 3) % 4) * 2 + y
     other_y = x * 2 + 1 - y
     b_p = other_y
-    b_far = ((x + 2) % 4) * 2 + y
-
-    def half_on(c, h, to):
-        rows = g.at[c, right if h else left, pl.ds(h * (R // 2), R // 2)]
-        return remote(rows, rows, g_ss, g_rs.at[c, 2], seq, to)
+    b_l0 = left
+    b_r1 = ((x + 1) % 4) * 2 + 1 - y
 
     def move(c, blk, role, to):
         return remote(g.at[c, blk], g.at[c, blk], g_ss, g_rs.at[c, role], seq, to)
@@ -204,7 +201,7 @@
     def send_chunk(c):
         move(c, tp, 0, other_y).start()
         move(c, tp, 1, right).start()
-        move(c, tp, 1, left).start()
+        move(c, tp, 3, left).start()
 
     make_chunk(0)
     for c in range(NC):
@@ -258,7 +255,7 @@
     def hand_on(i):
         arrived(i, 0, 1)
         move(i, b_p, 3, right).start()
-        move(i, b_p, 3, left).start()
+        move(i, b_p, 2, left).start()
 
     for c in range(HANDED):
         hand_on(c)
@@ -274,20 +271,16 @@
 
         @pl.when(i < NC)
         def _():
-            arrived(i, 1, 2)
-            half_on(i, 0, right).start()
-            half_on(i, 1, left).start()
-
-        @pl.when((i >= 1) & (i <= NC))
-        def _():
-            arrived(i - 1, 2, 1)
-            move(i - 1, b_far, 3, other_y).start()
+            arrived(i, 1, 1)
+            move(i, b_l0, 3, right).start()
+            arrived(i, 2, 1)
+            move(i, b_r1, 3, left).start()
 
     def projected(c0):
         for e in range(2):
             c = c0 + e
             rows = slice(e * R, (e + 1) * R)
-            arrived(c, 3, 3)
+            arrived(c, 3, 4)
             ss = jnp.zeros((R, 128), F32)
             for b in range(8):
                 g32 = g[c, b].astype(F32)
@@ -311,6 +304,14 @@
         for e in range(2):
             for d in (2, 1, 3):
                 spread(c0 + e, d).start()
+
+        @pl.when(yhi == 0)
+        def _():
+            for e in range(2):
+                cross(c0 + e, 0).start()
+
+        for e in range(2):
+            twin(c0 + e, 0).start()
         project(2, 0)
         for e in range(2):
             for d in (2, 1, 3):
@@ -318,7 +319,7 @@
 
     def share(c):
         spread_in(c)
-        for d in range(4):
+        for d in range(1, 4):
 
             @pl.when(yhi == 0)
             def _():
@@ -394,7 +395,9 @@
     ztot = ztot * inv_rms + bias_col
     post = 2.0 / (1.0 + jnp.exp(-ztot[0:8]))
     e0, e1 = balanced(jnp.exp(ztot[8:16]), jnp.exp(ztot[16:24]))
-    mix_cols[...] = columns(jnp.concatenate([post, e0, e1], axis=0))
+    cols[...] = columns(jnp.concatenate([post, e0, e1], axis=0))
+    noted = pltpu.make_async_copy(cols, mix_cols, m_sem)
+    noted.start()
 
     @pl.when(yhi == 1)
     def _():
@@ -402,6 +405,7 @@
         share_far(NC - 1)
 
     told.wait()
+    noted.wait()
     kept().wait()
 
     def all_of(ref, ssem, rsem):
@@ -531,7 +535,7 @@
             return c
 
         def two(k, c):
-            block(mid + 2 * k, "all", 2)
+            block(mid + 4 * k, "all", 4)
             return c
 
         def one(kb, c):
@@ -541,9 +545,9 @@
         block(qb, "diagonal")
         lax.fori_loop(jnp.where(qi == 0, first_needed, qb - 1), qb, land, 0)
         lax.fori_loop(lo, mid, some, 0)
-        pairs = (qb - mid) // 2
+        pairs = (qb - mid) // 4
         lax.fori_loop(0, pairs, two, 0)
-        lax.fori_loop(mid + 2 * pairs, qb, one, 0)
+        lax.fori_loop(mid + 4 * pairs, qb, one, 0)
         out = acc_ref[:, 0:HD] / acc_ref[:, HD : HD + 1]
         ctx[qi] = out.astype(BF).reshape(NO, RO, HD)
         return carry
@@ -693,7 +697,7 @@
             sds((TILES, 8, 128), jnp.int32),
         ),
         in_specs=[hbm] * 6,
-        out_specs=(hbm, vm, hbm),
+        out_specs=(hbm, hbm, hbm),
         scratch_shapes=[
             VMEM((T, S, W), BF),
             VMEM((S, T, W), BF),
@@ -713,6 +717,7 @@
             VMEM((4, 8, 128), jnp.int32),
             VMEM((5, 8, 128), jnp.int32),
             VMEM((T, 128), F32),
+            VMEM((T, 128), F32),
             DMA((4,)),
             DMA((4,)),
             DMA(()),
@@ -721,6 +726,7 @@
             DMA(()), DMA((3,)),
             DMA(()), DMA((NC, 4)),
             DMA(()), DMA((NC,)),
+            DMA(()),
             DMA(()),
             DMA(()),
             DMA(()),

time: 134 us -> 117 us (0.87)
  Pallas kernels: 132 us -> 116 us
    pallas_call x1, Pallas kernels: 80.2 us -> 63.2 us  [local(): pl.pallas_call(first_kernel, name='gather_project', out_shape=(sds((BLOCK...]
    pallas_call x1, Pallas kernels: 14.9 us -> 19.3 us  [local(): pl.pallas_call(attention_kernel, name='attention', out_shape=sds((4, NO,...]
    pallas_call x1, Pallas kernels: 35.8 us -> 32.5 us  [local(): pl.pallas_call(last_kernel, name='project_out', out_shape=sds((T, S, W),...]
where the time goes in v4:
time: 117 us; the launch traced here: 116 us
  Pallas kernels  116 us (99%)
    pallas_call x1, Pallas kernels, local(): pl.pallas_call(first_kernel, name='gather_project', out_shape=(sds((BLOCK...  63.2 us
    pallas_call x1, Pallas kernels, local(): pl.pallas_call(last_kernel, name='project_out', out_shape=sds((T, S, W),...  32.5 us
    pallas_call x1, Pallas kernels, local(): pl.pallas_call(attention_kernel, name='attention', out_shape=sds((4, NO,...  19.3 us

profile of v4, /device:TPU:25, one launch (start us, length us, event | category | flops | bytes accessed | tf_op | source)
XLA Modules:
  0.0 116.4 jit_solution(1326602080973730457)
XLA Ops:
  0.0 63.2 %gather_project.1 = (bf16[160,8,3,64,128]{4,3,2,1,0:T(8,128)(2,1)}, f32[512,128]{1,0:T(8,128)}, s32[9216,8,128]{2,1,0:T(8,128)}) custom-call(bf16[512,4,512]{2,1,0:T(4,128)(2,1)} %xraw.1, s32[4,128]{1,0:T(4,128)} %bitcast.8, f32[4,24,512]{2,1,0:T(8,128)} %bitcast.6, f32[1,24]{1,0:T(1,128)} %bitcast.9, f32[1,4096]{1,0:T(1,128)} %bitcast.7, ...), custom_call_target="tpu_custom_call" | custom-call | tf_op jit(solution)/shard_map/gather_project/pallas_call | solution.py:691
  63.2 0.0 copy-start
  63.2 0.0 copy-start.1
  63.2 0.0 copy-start.2
  63.2 19.3 %attention.1.ctx = bf16[4,4,128,128]{3,2,1,0:T(8,128)(2,1)S(1)} custom-call(bf16[160,8,3,64,128]{4,3,2,1,0:T(8,128)(2,1)} %get-tuple-element.8.att_hbm, s32[9216,8,128]{2,1,0:T(8,128)} %get-tuple-element.9.cnt_hbm), custom_call_target="tpu_custom_call" | custom-call | tf_op jit(solution)/shard_map/attention/pallas_call | solution.py:743
  82.5 0.0 copy-done
  82.6 0.0 copy-done.1
  82.6 0.0 copy-done.2
  82.6 32.5 %project_out.1.x = bf16[512,4,512]{2,1,0:T(4,128)(2,1)S(1)} custom-call(bf16[4,4,128,128]{3,2,1,0:T(8,128)(2,1)S(1)} %attention.1.ctx, bf16[512,4096]{1,0:T(8,128)(2,1)S(1)} %copy-done.1, bf16[512,4,512]{2,1,0:T(4,128)(2,1)S(1)} %copy-done, f32[512,128]{1,0:T(8,128)S(1)} %copy-done.2), custom_call_target="tpu_custom_call" | custom-call | tf_op jit(solution)/shard_map/project_out/pallas_call | solution.py:758
  115.1 1.3 %store.1 = bf16[512,4,512]{2,1,0:T(4,128)(2,1)} custom-call(bf16[512,4,512]{2,1,0:T(4,128)(2,1)S(1)} %project_out.1.x), custom_call_target="tpu_custom_call" | custom-call | tf_op jit(solution)/shard_map/store/pallas_call | solution.py:780
Async XLA Ops:
  63.2 19.4 %copy-start = (bf16[512,4,512]{2,1,0:T(4,128)(2,1)S(1)}, bf16[512,4,512]{2,1,0:T(4,128)(2,1)}, u32[]{:S(2)}) copy-start(bf16[512,4,512]{2,1,0:T(4,128)(2,1)} %xraw.1) | copy-start | bytes 6291460
  63.2 19.4 %copy-start.1 = (bf16[512,4096]{1,0:T(8,128)(2,1)S(1)}, bf16[512,4096]{1,0:T(8,128)(2,1)}, u32[]{:S(2)}) copy-start(bf16[512,4096]{1,0:T(8,128)(2,1)} %wbuf.1) | copy-start | bytes 12582916
  63.2 19.4 %copy-start.2 = (f32[512,128]{1,0:T(8,128)S(1)}, f32[512,128]{1,0:T(8,128)}, u32[]{:S(2)}) copy-start(f32[512,128]{1,0:T(8,128)} %get-tuple-element.10.cols) | copy-start | bytes 786436

commit v5 on v4

--- a/solution.py
+++ b/solution.py
@@ -221,12 +221,12 @@
     def spread(c, d):
         return remote(
             sb.at[(z + d) % 4, c, two], att.at[seq, c, two],
-            a_ss, a_rs.at[c], z_peers[d - 1], tp,
+            a_ss, a_rs.at[c, d - 1], z_peers[d - 1], tp,
         )
 
-    def spread_in(c):
-        ref = sb.at[pl.ds(0, 3), c, two]
-        remote(ref, ref, a_ss, a_rs.at[c], z_peers[0], tp).wait_recv()
+    def spread_in(c, d):
+        ref = sb.at[0, c, two]
+        remote(ref, ref, a_ss, a_rs.at[c, d - 1], z_peers[0], tp).wait_recv()
 
     def spread_q(c, d):
         return remote(
@@ -302,7 +302,7 @@
         project(0, 1)
         project(1, 2)
         for e in range(2):
-            for d in (2, 1, 3):
+            for d in (1, 3, 2):
                 spread(c0 + e, d).start()
 
         @pl.when(yhi == 0)
@@ -318,8 +318,8 @@
                 spread_q(c0 + e, d).start()
 
     def share(c):
-        spread_in(c)
-        for d in range(1, 4):
+        for d in (1, 3, 2):
+            spread_in(c, d)
 
             @pl.when(yhi == 0)
             def _():
@@ -416,7 +416,7 @@
     all_of(three, n_ss.at[1], n_rs.at[1]).wait_send()
     all_of(crecv, c_ss, c_rs.at[0]).wait_send()
     all_of(g.at[pl.ds(0, 7)], g_ss, g_rs.at[0, 0]).wait_send()
-    all_of(sb.at[pl.ds(0, 3)], a_ss, a_rs.at[0]).wait_send()
+    all_of(sb.at[pl.ds(0, 3)], a_ss, a_rs.at[0, 0]).wait_send()
     all_of(sb.at[pl.ds(0, 3), :, 2], a_ss, q_rs).wait_recv()
     twins = all_of(sb.at[:, :, two], sib_ss, sib_rs)
     twins.wait_send()
@@ -725,7 +725,7 @@
             DMA((2,)), DMA((2,)),
             DMA(()), DMA((3,)),
             DMA(()), DMA((NC, 4)),
-            DMA(()), DMA((NC,)),
+            DMA(()), DMA((NC, 3)),
             DMA(()),
             DMA(()),
             DMA(()),

time: 117 us -> 115 us (0.983)
  the two profiles are of different devices: /device:TPU:25 before, /device:TPU:24 now
where the time goes in v5:
time: 115 us; the launch traced here: 114 us
  Pallas kernels  114 us (99%)
    pallas_call x1, Pallas kernels, local(): pl.pallas_call(first_kernel, name='gather_project', out_shape=(sds((BLOCK...  62.3 us
    pallas_call x1, Pallas kernels, local(): pl.pallas_call(last_kernel, name='project_out', out_shape=sds((T, S, W),...  33.2 us
    pallas_call x1, Pallas kernels, local(): pl.pallas_call(attention_kernel, name='attention', out_shape=sds((4, NO,...  17.4 us

profile of v5, /device:TPU:24, one launch (start us, length us, event | category | flops | bytes accessed | tf_op | source)
XLA Modules:
  0.0 114.4 jit_solution(14588637250239212923)
XLA Ops:
  0.0 62.3 %gather_project.1 = (bf16[160,8,3,64,128]{4,3,2,1,0:T(8,128)(2,1)}, f32[512,128]{1,0:T(8,128)}, s32[9216,8,128]{2,1,0:T(8,128)}) custom-call(bf16[512,4,512]{2,1,0:T(4,128)(2,1)} %xraw.1, s32[4,128]{1,0:T(4,128)} %bitcast.8, f32[4,24,512]{2,1,0:T(8,128)} %bitcast.6, f32[1,24]{1,0:T(1,128)} %bitcast.9, f32[1,4096]{1,0:T(1,128)} %bitcast.7, ...), custom_call_target="tpu_custom_call" | custom-call | tf_op jit(solution)/shard_map/gather_project/pallas_call | solution.py:691
  62.3 0.0 copy-start
  62.3 0.0 copy-start.1
  62.3 0.0 copy-start.2
  62.3 17.4 %attention.1.ctx = bf16[4,4,128,128]{3,2,1,0:T(8,128)(2,1)S(1)} custom-call(bf16[160,8,3,64,128]{4,3,2,1,0:T(8,128)(2,1)} %get-tuple-element.8.att_hbm, s32[9216,8,128]{2,1,0:T(8,128)} %get-tuple-element.9.cnt_hbm), custom_call_target="tpu_custom_call" | custom-call | tf_op jit(solution)/shard_map/attention/pallas_call | solution.py:743
  79.7 0.0 copy-done
  79.7 0.0 copy-done.1
  79.7 0.0 copy-done.2
  79.7 33.2 %project_out.1.x = bf16[512,4,512]{2,1,0:T(4,128)(2,1)S(1)} custom-call(bf16[4,4,128,128]{3,2,1,0:T(8,128)(2,1)S(1)} %attention.1.ctx, bf16[512,4096]{1,0:T(8,128)(2,1)S(1)} %copy-done.1, bf16[512,4,512]{2,1,0:T(4,128)(2,1)S(1)} %copy-done, f32[512,128]{1,0:T(8,128)S(1)} %copy-done.2), custom_call_target="tpu_custom_call" | custom-call | tf_op jit(solution)/shard_map/project_out/pallas_call | solution.py:758
  113.0 1.3 %store.1 = bf16[512,4,512]{2,1,0:T(4,128)(2,1)} custom-call(bf16[512,4,512]{2,1,0:T(4,128)(2,1)S(1)} %project_out.1.x), custom_call_target="tpu_custom_call" | custom-call | tf_op jit(solution)/shard_map/store/pallas_call | solution.py:780
Async XLA Ops:
  62.3 17.4 %copy-start = (bf16[512,4,512]{2,1,0:T(4,128)(2,1)S(1)}, bf16[512,4,512]{2,1,0:T(4,128)(2,1)}, u32[]{:S(2)}) copy-start(bf16[512,4,512]{2,1,0:T(4,128)(2,1)} %xraw.1) | copy-start | bytes 6291460
  62.3 17.4 %copy-start.1 = (bf16[512,4096]{1,0:T(8,128)(2,1)S(1)}, bf16[512,4096]{1,0:T(8,128)(2,1)}, u32[]{:S(2)}) copy-start(bf16[512,4096]{1,0:T(8,128)(2,1)} %wbuf.1) | copy-start | bytes 12582916
  62.3 17.4 %copy-start.2 = (f32[512,128]{1,0:T(8,128)S(1)}, f32[512,128]{1,0:T(8,128)}, u32[]{:S(2)}) copy-start(f32[512,128]{1,0:T(8,128)} %get-tuple-element.10.cols) | copy-start | bytes 786436
